TPU v7x, 32 devices: a whole 2x2x4 slice. The times are simulated.
32 devices in a mesh: gx: 4 (over x, core), gy: 4 (over z), gz: 2 (over y).
Axes of the slice: x: 2, y: 2, z: 4, core: 2. Of those that a mesh axis runs over, the one named last changes fastest.
Arguments:
- density: float32 [32, 64, 256], P('gx', 'gy', 'gz'), may hold values from 0.1 to 10
- x_faces: float32 [2, 64, 256], P(None, 'gy', 'gz'), may hold values from -6 to 6
- y_faces: float32 [2, 32, 256], P(None, 'gx', 'gz'), may hold values from -6 to 6
- z_faces: float32 [2, 32, 64], P(None, 'gx', 'gy'), may hold values from -6 to 6
Outputs:
- solution_field: float32 [32, 64, 256], P('gx', 'gy', 'gz')
- residual: float32 [32, 64, 256], P('gx', 'gy', 'gz')
All inputs are finite; a program needn't handle non-finite values.
Results may differ from a plain program's by a relative error of at most 0.0003.
Values sent between devices are 32-bit elements; how exact they have to be, the bound alone decides.
A program may use at most 64 MiB of HBM per device.

v0:
```python
import jax
import jax.numpy as jnp
from jax import lax
from jax.sharding import PartitionSpec as P

ITERS = 2
LEVELS = 3
COARSE_SWEEPS = 3
relax_rate = 1.0 / 9.0
coupling = 0.5


def padded_2(cells, sides, width):
    for axis, dim in sides:
        count = lax.axis_size(axis)
        ends = count - 1
        head = lax.slice_in_dim(cells, 0, width, axis=dim)
        tail = lax.slice_in_dim(cells, cells.shape[dim] - width, cells.shape[dim], axis=dim)
        cells = jnp.concatenate(
            [
                lax.ppermute(tail, axis, [(i, (i + 1) % count) for i in range(ends)]),
                cells,
                lax.ppermute(head, axis, [((i + 1) % count, i) for i in range(ends)]),
            ],
            axis=dim,
        )
    return cells


def beside_sum(padded):
    beside = padded[2:, 1:-1, 1:-1] + padded[:-2, 1:-1, 1:-1]
    beside = beside + padded[1:-1, 2:, 1:-1] + padded[1:-1, :-2, 1:-1]
    beside = beside + padded[1:-1, 1:-1, 2:] + padded[1:-1, 1:-1, :-2]
    return beside


def operate(field):
    padded = padded_2(field, (("gx", 0), ("gy", 1), ("gz", 2)), 1)
    return 6.0 * field - beside_sum(padded)


def restrict(field):
    sx, sy, sz = field.shape
    return 0.5 * jnp.sum(field.reshape(sx // 2, 2, sy // 2, 2, sz // 2, 2), axis=(1, 3, 5))


def prolong(field):
    sx, sy, sz = field.shape
    spread = jnp.broadcast_to(field[:, None, :, None, :, None], (sx, 2, sy, 2, sz, 2))
    return spread.reshape(2 * sx, 2 * sy, 2 * sz)


def coarse_solve(right_side):
    approx = relax_rate * right_side
    for sweep_idx in range(COARSE_SWEEPS - 1):
        approx = approx + relax_rate * (right_side - operate(approx))
    return approx


def cycle(right_side, level_idx):
    if level_idx == LEVELS - 1:
        return coarse_solve(right_side)
    approx = relax_rate * right_side
    defect = right_side - operate(approx)
    approx = approx + prolong(cycle(restrict(defect), level_idx + 1))
    return approx + relax_rate * (right_side - operate(approx))


def precondition_image(residual):
    approx = relax_rate * residual
    defect = residual - operate(approx)
    approx = approx + prolong(cycle(restrict(defect), 1))
    precond = approx + relax_rate * (residual - operate(approx))
    return (precond, operate(precond))


def joint_sums(residual, precond, precond_image):
    return lax.psum(
        (jnp.sum(residual * precond), jnp.sum(precond * precond_image)), ("gx", "gy", "gz")
    )


def local(density, x_faces, y_faces, z_faces):
    right_side = -coupling * density
    right_side = right_side.at[0].add(jnp.where(lax.axis_index("gx") == 0, x_faces[0], 0.0))
    right_side = right_side.at[-1].add(
        jnp.where(lax.axis_index("gx") == lax.axis_size("gx") - 1, x_faces[1], 0.0)
    )
    right_side = right_side.at[:, 0].add(jnp.where(lax.axis_index("gy") == 0, y_faces[0], 0.0))
    right_side = right_side.at[:, -1].add(
        jnp.where(lax.axis_index("gy") == lax.axis_size("gy") - 1, y_faces[1], 0.0)
    )
    right_side = right_side.at[:, :, 0].add(jnp.where(lax.axis_index("gz") == 0, z_faces[0], 0.0))
    right_side = right_side.at[:, :, -1].add(
        jnp.where(lax.axis_index("gz") == lax.axis_size("gz") - 1, z_faces[1], 0.0)
    )
    solution_field = jnp.zeros_like(right_side)
    residual = right_side
    precond, pimage = precondition_image(residual)
    gamma_now, delta_now = joint_sums(residual, precond, pimage)
    step_size = gamma_now / delta_now
    direction = precond
    image = pimage
    for iteration in range(ITERS):
        solution_field = solution_field + step_size * direction
        residual = residual - step_size * image
        if iteration + 1 < ITERS:
            precond, pimage = precondition_image(residual)
            gamma_next, delta_now = joint_sums(residual, precond, pimage)
            growth = gamma_next / gamma_now
            step_size = gamma_next / (delta_now - growth * gamma_next / step_size)
            direction = precond + growth * direction
            image = pimage + growth * image
            gamma_now = gamma_next
    return (solution_field, residual)


def solution(mesh):
    placed = (P("gx", "gy", "gz"), P(None, "gy", "gz"), P(None, "gx", "gz"), P(None, "gx", "gy"))
    return jax.shard_map(
        local,
        mesh=mesh,
        in_specs=placed,
        out_specs=(P("gx", "gy", "gz"), P("gx", "gy", "gz")),
        check_vma=False,
    )
```

profile of v0, /device:TPU:0, one launch (start us, length us, event | category | flops | bytes accessed | tf_op | source)
XLA Modules:
  0.0 447.0 jit_solution(14585865203178151071)
XLA Ops:
  5.6 2.4 collective-permute-start.1
  9.3 3.9 collective-permute-done
  13.2 3.5 collective-permute-start.3
  18.0 4.2 collective-permute-done.2
  23.6 4.6 %collective-permute-start.5 = (f32[10,18,1]{2,1,0:T(8,128)S(1)}, f32[10,18,1]{2,1,0:T(8,128)S(1)}, u32[]{:S(2)}, u32[]{:S(2)}) collective-permute-start(f32[10,18,1]{2,1,0:T(8,128)S(1)} %get-tuple-element.101), channel_id=1, source_target_pairs={{0,1},{2,3},{4,5},{6,7},{8,9},{10,11},{12,13},{14,15},{16,17},{18,... | collective-permute-start | bytes 2168 | tf_op jit(solution)/shard_map/ppermute | solution.py:21
  28.2 2.2 collective-permute-done.4
  31.7 5.5 %reshape.240 = f32[4,2,8,2,64,2]{5,4,3,2,1,0:T(8,128)} reshape(f32[8,16,128]{2,1,0:T(8,128)S(1)} %fusion.39) | data formatting | bytes 131072 | tf_op jit(solution)/shard_map/reshape | solution.py:44
  37.2 2.5 reduce_sum.72
  42.9 2.9 collective-permute-done.6
  45.8 3.5 collective-permute-start.9
  50.6 4.2 collective-permute-done.8
  56.1 4.5 %collective-permute-start.11 = (f32[6,10,1]{2,1,0:T(8,128)S(1)}, f32[6,10,1]{2,1,0:T(8,128)S(1)}, u32[]{:S(2)}, u32[]{:S(2)}) collective-permute-start(f32[6,10,1]{2,1,0:T(8,128)S(1)} %get-tuple-element.133), channel_id=1, source_target_pairs={{0,1},{2,3},{4,5},{6,7},{8,9},{10,11},{12,13},{14,15},{16,17},{18,... | collective-permute-start | bytes 728 | tf_op jit(solution)/shard_map/ppermute | solution.py:21
  66.4 3.6 collective-permute-done.12
  70.1 3.5 collective-permute-start.15
  74.9 4.2 collective-permute-done.14
  80.4 4.5 %collective-permute-start.17 = (f32[4,6,1]{2,1,0:T(8,128)S(1)}, f32[4,6,1]{2,1,0:T(8,128)S(1)}, u32[]{:S(2)}, u32[]{:S(2)}) collective-permute-start(f32[4,6,1]{2,1,0:T(8,128)S(1)} %get-tuple-element.155), channel_id=1, source_target_pairs={{0,1},{2,3},{4,5},{6,7},{8,9},{10,11},{12,13},{14,15},{16,17},{18,... | collective-permute-start | bytes 296 | tf_op jit(solution)/shard_map/ppermute | solution.py:21
  89.5 3.8 collective-permute-done.18
  96.6 4.2 collective-permute-done.20
  102.2 4.5 %collective-permute-start.23 = (f32[4,6,1]{2,1,0:T(8,128)S(1)}, f32[4,6,1]{2,1,0:T(8,128)S(1)}, u32[]{:S(2)}, u32[]{:S(2)}) collective-permute-start(f32[4,6,1]{2,1,0:T(8,128)S(1)} %get-tuple-element.153), channel_id=1, source_target_pairs={{0,1},{2,3},{4,5},{6,7},{8,9},{10,11},{12,13},{14,15},{16,17},{18,... | collective-permute-start | bytes 296 | tf_op jit(solution)/shard_map/ppermute | solution.py:21
  111.7 3.8 collective-permute-done.24
  118.8 4.2 collective-permute-done.26
  124.3 4.5 %collective-permute-start.29 = (f32[6,10,1]{2,1,0:T(8,128)S(1)}, f32[6,10,1]{2,1,0:T(8,128)S(1)}, u32[]{:S(2)}, u32[]{:S(2)}) collective-permute-start(f32[6,10,1]{2,1,0:T(8,128)S(1)} %get-tuple-element.131), channel_id=1, source_target_pairs={{0,1},{2,3},{4,5},{6,7},{8,9},{10,11},{12,13},{14,15},{16,17},{18,... | collective-permute-start | bytes 728 | tf_op jit(solution)/shard_map/ppermute | solution.py:21
  130.8 2.6 broadcast_in_dim.43
  133.4 4.0 reshape.243
  140.4 3.9 collective-permute-done.30
  147.5 4.2 collective-permute-done.32
  153.1 4.6 %collective-permute-start.35 = (f32[10,18,1]{2,1,0:T(8,128)S(1)}, f32[10,18,1]{2,1,0:T(8,128)S(1)}, u32[]{:S(2)}, u32[]{:S(2)}) collective-permute-start(f32[10,18,1]{2,1,0:T(8,128)S(1)} %get-tuple-element.99), channel_id=1, source_target_pairs={{0,1},{2,3},{4,5},{6,7},{8,9},{10,11},{12,13},{14,15},{16,17},{18,... | collective-permute-start | bytes 2168 | tf_op jit(solution)/shard_map/ppermute | solution.py:21
  157.7 2.2 collective-permute-done.34
  164.3 2.9 collective-permute-done.36
  170.4 4.2 collective-permute-done.38
  176.1 4.6 %collective-permute-start.41 = (f32[10,18,1]{2,1,0:T(8,128)S(1)}, f32[10,18,1]{2,1,0:T(8,128)S(1)}, u32[]{:S(2)}, u32[]{:S(2)}) collective-permute-start(f32[10,18,1]{2,1,0:T(8,128)S(1)} %get-tuple-element.97), channel_id=1, source_target_pairs={{0,1},{2,3},{4,5},{6,7},{8,9},{10,11},{12,13},{14,15},{16,17},{18,... | collective-permute-start | bytes 2168 | tf_op jit(solution)/shard_map/ppermute | solution.py:21
  180.6 2.1 collective-permute-done.40
  184.9 39.6 %all-reduce.1 = (f32[]{:T(128)}, f32[]{:T(128)}) all-reduce(f32[]{:T(128)} %get-tuple-element.81, f32[]{:T(128)} %get-tuple-element.80), channel_id=1, replica_groups=mesh['gx'=4,'gy'=4,'gz'=2] {'gx','gy','gz'}, use_global_device_ids=true, to_apply=%region_3.4 | all-reduce | flops 2 | bytes 16 | tf_op jit(solution)/shard_map/psum | solution.py:78
  228.4 4.3 collective-permute-done.42
  232.7 3.9 collective-permute-start.45
  237.9 4.2 collective-permute-done.44
  243.6 4.6 %collective-permute-start.47 = (f32[10,18,1]{2,1,0:T(8,128)S(1)}, f32[10,18,1]{2,1,0:T(8,128)S(1)}, u32[]{:S(2)}, u32[]{:S(2)}) collective-permute-start(f32[10,18,1]{2,1,0:T(8,128)S(1)} %get-tuple-element.95), channel_id=1, source_target_pairs={{0,1},{2,3},{4,5},{6,7},{8,9},{10,11},{12,13},{14,15},{16,17},{18,... | collective-permute-start | bytes 2168 | tf_op jit(solution)/shard_map/ppermute | solution.py:21
  248.1 2.2 collective-permute-done.46
  251.7 5.5 %reshape.244 = f32[4,2,8,2,64,2]{5,4,3,2,1,0:T(8,128)} reshape(f32[8,16,128]{2,1,0:T(8,128)S(1)} %fusion.17) | data formatting | bytes 131072 | tf_op jit(solution)/shard_map/reshape | solution.py:44
  257.2 2.5 reduce_sum.76
  262.8 2.9 collective-permute-done.48
  265.7 2.6 collective-permute-start.51
  269.6 4.2 collective-permute-done.50
  275.2 4.7 %collective-permute-start.53 = (f32[6,10,1]{2,1,0:T(8,128)S(1)}, f32[6,10,1]{2,1,0:T(8,128)S(1)}, u32[]{:S(2)}, u32[]{:S(2)}) collective-permute-start(f32[6,10,1]{2,1,0:T(8,128)S(1)} %get-tuple-element.129), channel_id=1, source_target_pairs={{0,1},{2,3},{4,5},{6,7},{8,9},{10,11},{12,13},{14,15},{16,17},{18,... | collective-permute-start | bytes 728 | tf_op jit(solution)/shard_map/ppermute | solution.py:21
  285.5 3.6 collective-permute-done.54
  292.4 4.2 collective-permute-done.56
  297.9 4.5 %collective-permute-start.59 = (f32[4,6,1]{2,1,0:T(8,128)S(1)}, f32[4,6,1]{2,1,0:T(8,128)S(1)}, u32[]{:S(2)}, u32[]{:S(2)}) collective-permute-start(f32[4,6,1]{2,1,0:T(8,128)S(1)} %get-tuple-element.147), channel_id=1, source_target_pairs={{0,1},{2,3},{4,5},{6,7},{8,9},{10,11},{12,13},{14,15},{16,17},{18,... | collective-permute-start | bytes 296 | tf_op jit(solution)/shard_map/ppermute | solution.py:21
  307.0 3.8 collective-permute-done.60
  314.1 4.2 collective-permute-done.62
  319.6 4.5 %collective-permute-start.65 = (f32[4,6,1]{2,1,0:T(8,128)S(1)}, f32[4,6,1]{2,1,0:T(8,128)S(1)}, u32[]{:S(2)}, u32[]{:S(2)}) collective-permute-start(f32[4,6,1]{2,1,0:T(8,128)S(1)} %get-tuple-element.145), channel_id=1, source_target_pairs={{0,1},{2,3},{4,5},{6,7},{8,9},{10,11},{12,13},{14,15},{16,17},{18,... | collective-permute-start | bytes 296 | tf_op jit(solution)/shard_map/ppermute | solution.py:21
  329.1 3.8 collective-permute-done.66
  336.2 4.2 collective-permute-done.68
  341.8 4.5 %collective-permute-start.71 = (f32[6,10,1]{2,1,0:T(8,128)S(1)}, f32[6,10,1]{2,1,0:T(8,128)S(1)}, u32[]{:S(2)}, u32[]{:S(2)}) collective-permute-start(f32[6,10,1]{2,1,0:T(8,128)S(1)} %get-tuple-element.127), channel_id=1, source_target_pairs={{0,1},{2,3},{4,5},{6,7},{8,9},{10,11},{12,13},{14,15},{16,17},{18,... | collective-permute-start | bytes 728 | tf_op jit(solution)/shard_map/ppermute | solution.py:21
  348.3 2.6 broadcast_in_dim.45
  350.9 4.0 reshape.247
  357.9 3.9 collective-permute-done.72
  365.0 4.2 collective-permute-done.74
  370.6 4.6 %collective-permute-start.77 = (f32[10,18,1]{2,1,0:T(8,128)S(1)}, f32[10,18,1]{2,1,0:T(8,128)S(1)}, u32[]{:S(2)}, u32[]{:S(2)}) collective-permute-start(f32[10,18,1]{2,1,0:T(8,128)S(1)} %get-tuple-element.93), channel_id=1, source_target_pairs={{0,1},{2,3},{4,5},{6,7},{8,9},{10,11},{12,13},{14,15},{16,17},{18,... | collective-permute-start | bytes 2168 | tf_op jit(solution)/shard_map/ppermute | solution.py:21
  375.2 2.2 collective-permute-done.76
  381.8 2.9 collective-permute-done.78
  387.9 4.2 collective-permute-done.80
  393.5 4.6 %collective-permute-start.83 = (f32[10,18,1]{2,1,0:T(8,128)S(1)}, f32[10,18,1]{2,1,0:T(8,128)S(1)}, u32[]{:S(2)}, u32[]{:S(2)}) collective-permute-start(f32[10,18,1]{2,1,0:T(8,128)S(1)} %get-tuple-element.91), channel_id=1, source_target_pairs={{0,1},{2,3},{4,5},{6,7},{8,9},{10,11},{12,13},{14,15},{16,17},{18,... | collective-permute-start | bytes 2168 | tf_op jit(solution)/shard_map/ppermute | solution.py:21
  398.1 2.1 collective-permute-done.82
  402.4 39.6 %all-reduce = (f32[]{:T(128)}, f32[]{:T(128)}) all-reduce(f32[]{:T(128)} %get-tuple-element.79, f32[]{:T(128)} %get-tuple-element.78), channel_id=1, replica_groups=mesh['gx'=4,'gy'=4,'gz'=2] {'gx','gy','gz'}, use_global_device_ids=true, to_apply=%region_9.10 | all-reduce | flops 2 | bytes 16 | tf_op jit(solution)/shard_map/psum | solution.py:78
  (218 shorter events, 125.9 us)
Async XLA Ops:
  5.6 3.7 collective-permute-start.1
  8.0 5.2 %collective-permute-start = (f32[1,16,128]{2,1,0:T(8,128)S(1)}, f32[1,16,128]{2,1,0:T(8,128)S(1)}, u32[]{:S(2)}, u32[]{:S(2)}) collective-permute-start(f32[1,16,128]{2,1,0:T(8,128)S(1)} %get-tuple-element.125), channel_id=1, source_target_pairs={{8,0},{16,8},{24,16},{9,1},{17,9},{25,17},{10,2},{18,10},{26,18},{... | collective-permute-start | bytes 24584 | tf_op jit(solution)/shard_map/ppermute | solution.py:23
  13.2 4.8 %collective-permute-start.3 = (f32[10,1,128]{2,1,0:T(1,128)S(1)}, f32[10,1,128]{2,1,0:T(1,128)S(1)}, u32[]{:S(2)}, u32[]{:S(2)}) collective-permute-start(f32[10,1,128]{2,1,0:T(1,128)S(1)} %get-tuple-element.112), channel_id=1, source_target_pairs={{0,2},{2,4},{4,6},{1,3},{3,5},{5,7},{8,10},{10,12},{12,14},{9,11},... | collective-permute-start | bytes 15368 | tf_op jit(solution)/shard_map/ppermute | solution.py:21
  16.7 5.5 %collective-permute-start.2 = (f32[10,1,128]{2,1,0:T(1,128)S(1)}, f32[10,1,128]{2,1,0:T(1,128)S(1)}, u32[]{:S(2)}, u32[]{:S(2)}) collective-permute-start(f32[10,1,128]{2,1,0:T(1,128)S(1)} %get-tuple-element.113), channel_id=1, source_target_pairs={{2,0},{4,2},{6,4},{3,1},{5,3},{7,5},{10,8},{12,10},{14,12},{11,9},... | collective-permute-start | bytes 15368 | tf_op jit(solution)/shard_map/ppermute | solution.py:23
  22.3 8.1 %collective-permute-start.4 = (f32[10,18,1]{2,1,0:T(8,128)S(1)}, f32[10,18,1]{2,1,0:T(8,128)S(1)}, u32[]{:S(2)}, u32[]{:S(2)}) collective-permute-start(f32[10,18,1]{2,1,0:T(8,128)S(1)} %get-tuple-element.100), channel_id=1, source_target_pairs={{1,0},{3,2},{5,4},{7,6},{9,8},{11,10},{13,12},{15,14},{17,16},{19,... | collective-permute-start | bytes 2168 | tf_op jit(solution)/shard_map/ppermute | solution.py:23
  23.6 8.0 %collective-permute-start.5 = (f32[10,18,1]{2,1,0:T(8,128)S(1)}, f32[10,18,1]{2,1,0:T(8,128)S(1)}, u32[]{:S(2)}, u32[]{:S(2)}) collective-permute-start(f32[10,18,1]{2,1,0:T(8,128)S(1)} %get-tuple-element.101), channel_id=1, source_target_pairs={{0,1},{2,3},{4,5},{6,7},{8,9},{10,11},{12,13},{14,15},{16,17},{18,... | collective-permute-start | bytes 2168 | tf_op jit(solution)/shard_map/ppermute | solution.py:21
  41.6 4.2 collective-permute-start.6
  45.8 4.8 %collective-permute-start.9 = (f32[6,1,64]{2,1,0:T(1,128)S(1)}, f32[6,1,64]{2,1,0:T(1,128)S(1)}, u32[]{:S(2)}, u32[]{:S(2)}) collective-permute-start(f32[6,1,64]{2,1,0:T(1,128)S(1)} %get-tuple-element.140), channel_id=1, source_target_pairs={{0,2},{2,4},{4,6},{1,3},{3,5},{5,7},{8,10},{10,12},{12,14},{9,11},... | collective-permute-start | bytes 4616 | tf_op jit(solution)/shard_map/ppermute | solution.py:21
  49.2 5.5 %collective-permute-start.8 = (f32[6,1,64]{2,1,0:T(1,128)S(1)}, f32[6,1,64]{2,1,0:T(1,128)S(1)}, u32[]{:S(2)}, u32[]{:S(2)}) collective-permute-start(f32[6,1,64]{2,1,0:T(1,128)S(1)} %get-tuple-element.141), channel_id=1, source_target_pairs={{2,0},{4,2},{6,4},{3,1},{5,3},{7,5},{10,8},{12,10},{14,12},{11,9},... | collective-permute-start | bytes 4616 | tf_op jit(solution)/shard_map/ppermute | solution.py:23
  54.8 6.5 %collective-permute-start.10 = (f32[6,10,1]{2,1,0:T(8,128)S(1)}, f32[6,10,1]{2,1,0:T(8,128)S(1)}, u32[]{:S(2)}, u32[]{:S(2)}) collective-permute-start(f32[6,10,1]{2,1,0:T(8,128)S(1)} %get-tuple-element.132), channel_id=1, source_target_pairs={{1,0},{3,2},{5,4},{7,6},{9,8},{11,10},{13,12},{15,14},{17,16},{19,... | collective-permute-start | bytes 728 | tf_op jit(solution)/shard_map/ppermute | solution.py:23
  56.1 6.4 %collective-permute-start.11 = (f32[6,10,1]{2,1,0:T(8,128)S(1)}, f32[6,10,1]{2,1,0:T(8,128)S(1)}, u32[]{:S(2)}, u32[]{:S(2)}) collective-permute-start(f32[6,10,1]{2,1,0:T(8,128)S(1)} %get-tuple-element.133), channel_id=1, source_target_pairs={{0,1},{2,3},{4,5},{6,7},{8,9},{10,11},{12,13},{14,15},{16,17},{18,... | collective-permute-start | bytes 728 | tf_op jit(solution)/shard_map/ppermute | solution.py:21
  65.1 4.9 %collective-permute-start.12 = (f32[1,4,32]{2,1,0:T(4,128)S(1)}, f32[1,4,32]{2,1,0:T(4,128)S(1)}, u32[]{:S(2)}, u32[]{:S(2)}) collective-permute-start(f32[1,4,32]{2,1,0:T(4,128)S(1)} %get-tuple-element.177), channel_id=1, source_target_pairs={{8,0},{16,8},{24,16},{9,1},{17,9},{25,17},{10,2},{18,10},{26,18},{... | collective-permute-start | bytes 1544 | tf_op jit(solution)/shard_map/ppermute | solution.py:23
  70.1 4.8 %collective-permute-start.15 = (f32[4,1,32]{2,1,0:T(1,128)S(1)}, f32[4,1,32]{2,1,0:T(1,128)S(1)}, u32[]{:S(2)}, u32[]{:S(2)}) collective-permute-start(f32[4,1,32]{2,1,0:T(1,128)S(1)} %get-tuple-element.164), channel_id=1, source_target_pairs={{0,2},{2,4},{4,6},{1,3},{3,5},{5,7},{8,10},{10,12},{12,14},{9,11},... | collective-permute-start | bytes 1544 | tf_op jit(solution)/shard_map/ppermute | solution.py:21
  73.6 5.5 %collective-permute-start.14 = (f32[4,1,32]{2,1,0:T(1,128)S(1)}, f32[4,1,32]{2,1,0:T(1,128)S(1)}, u32[]{:S(2)}, u32[]{:S(2)}) collective-permute-start(f32[4,1,32]{2,1,0:T(1,128)S(1)} %get-tuple-element.165), channel_id=1, source_target_pairs={{2,0},{4,2},{6,4},{3,1},{5,3},{7,5},{10,8},{12,10},{14,12},{11,9},... | collective-permute-start | bytes 1544 | tf_op jit(solution)/shard_map/ppermute | solution.py:23
  79.1 5.8 %collective-permute-start.16 = (f32[4,6,1]{2,1,0:T(8,128)S(1)}, f32[4,6,1]{2,1,0:T(8,128)S(1)}, u32[]{:S(2)}, u32[]{:S(2)}) collective-permute-start(f32[4,6,1]{2,1,0:T(8,128)S(1)} %get-tuple-element.154), channel_id=1, source_target_pairs={{1,0},{3,2},{5,4},{7,6},{9,8},{11,10},{13,12},{15,14},{17,16},{19,... | collective-permute-start | bytes 296 | tf_op jit(solution)/shard_map/ppermute | solution.py:23
  80.4 6.0 %collective-permute-start.17 = (f32[4,6,1]{2,1,0:T(8,128)S(1)}, f32[4,6,1]{2,1,0:T(8,128)S(1)}, u32[]{:S(2)}, u32[]{:S(2)}) collective-permute-start(f32[4,6,1]{2,1,0:T(8,128)S(1)} %get-tuple-element.155), channel_id=1, source_target_pairs={{0,1},{2,3},{4,5},{6,7},{8,9},{10,11},{12,13},{14,15},{16,17},{18,... | collective-permute-start | bytes 296 | tf_op jit(solution)/shard_map/ppermute | solution.py:21
  88.2 5.2 %collective-permute-start.18 = (f32[1,4,32]{2,1,0:T(4,128)S(1)}, f32[1,4,32]{2,1,0:T(4,128)S(1)}, u32[]{:S(2)}, u32[]{:S(2)}) collective-permute-start(f32[1,4,32]{2,1,0:T(4,128)S(1)} %get-tuple-element.175), channel_id=1, source_target_pairs={{8,0},{16,8},{24,16},{9,1},{17,9},{25,17},{10,2},{18,10},{26,18},{... | collective-permute-start | bytes 1544 | tf_op jit(solution)/shard_map/ppermute | solution.py:23
  95.3 5.5 %collective-permute-start.20 = (f32[4,1,32]{2,1,0:T(1,128)S(1)}, f32[4,1,32]{2,1,0:T(1,128)S(1)}, u32[]{:S(2)}, u32[]{:S(2)}) collective-permute-start(f32[4,1,32]{2,1,0:T(1,128)S(1)} %get-tuple-element.163), channel_id=1, source_target_pairs={{2,0},{4,2},{6,4},{3,1},{5,3},{7,5},{10,8},{12,10},{14,12},{11,9},... | collective-permute-start | bytes 1544 | tf_op jit(solution)/shard_map/ppermute | solution.py:23
  100.9 5.8 %collective-permute-start.22 = (f32[4,6,1]{2,1,0:T(8,128)S(1)}, f32[4,6,1]{2,1,0:T(8,128)S(1)}, u32[]{:S(2)}, u32[]{:S(2)}) collective-permute-start(f32[4,6,1]{2,1,0:T(8,128)S(1)} %get-tuple-element.152), channel_id=1, source_target_pairs={{1,0},{3,2},{5,4},{7,6},{9,8},{11,10},{13,12},{15,14},{17,16},{19,... | collective-permute-start | bytes 296 | tf_op jit(solution)/shard_map/ppermute | solution.py:23
  102.2 6.0 %collective-permute-start.23 = (f32[4,6,1]{2,1,0:T(8,128)S(1)}, f32[4,6,1]{2,1,0:T(8,128)S(1)}, u32[]{:S(2)}, u32[]{:S(2)}) collective-permute-start(f32[4,6,1]{2,1,0:T(8,128)S(1)} %get-tuple-element.153), channel_id=1, source_target_pairs={{0,1},{2,3},{4,5},{6,7},{8,9},{10,11},{12,13},{14,15},{16,17},{18,... | collective-permute-start | bytes 296 | tf_op jit(solution)/shard_map/ppermute | solution.py:21
  110.4 5.2 %collective-permute-start.24 = (f32[1,8,64]{2,1,0:T(8,128)S(1)}, f32[1,8,64]{2,1,0:T(8,128)S(1)}, u32[]{:S(2)}, u32[]{:S(2)}) collective-permute-start(f32[1,8,64]{2,1,0:T(8,128)S(1)} %get-tuple-element.151), channel_id=1, source_target_pairs={{8,0},{16,8},{24,16},{9,1},{17,9},{25,17},{10,2},{18,10},{26,18},{... | collective-permute-start | bytes 6152 | tf_op jit(solution)/shard_map/ppermute | solution.py:23
  117.5 5.5 %collective-permute-start.26 = (f32[6,1,64]{2,1,0:T(1,128)S(1)}, f32[6,1,64]{2,1,0:T(1,128)S(1)}, u32[]{:S(2)}, u32[]{:S(2)}) collective-permute-start(f32[6,1,64]{2,1,0:T(1,128)S(1)} %get-tuple-element.139), channel_id=1, source_target_pairs={{2,0},{4,2},{6,4},{3,1},{5,3},{7,5},{10,8},{12,10},{14,12},{11,9},... | collective-permute-start | bytes 4616 | tf_op jit(solution)/shard_map/ppermute | solution.py:23
  123.0 6.5 %collective-permute-start.28 = (f32[6,10,1]{2,1,0:T(8,128)S(1)}, f32[6,10,1]{2,1,0:T(8,128)S(1)}, u32[]{:S(2)}, u32[]{:S(2)}) collective-permute-start(f32[6,10,1]{2,1,0:T(8,128)S(1)} %get-tuple-element.130), channel_id=1, source_target_pairs={{1,0},{3,2},{5,4},{7,6},{9,8},{11,10},{13,12},{15,14},{17,16},{19,... | collective-permute-start | bytes 728 | tf_op jit(solution)/shard_map/ppermute | solution.py:23
  124.3 6.4 %collective-permute-start.29 = (f32[6,10,1]{2,1,0:T(8,128)S(1)}, f32[6,10,1]{2,1,0:T(8,128)S(1)}, u32[]{:S(2)}, u32[]{:S(2)}) collective-permute-start(f32[6,10,1]{2,1,0:T(8,128)S(1)} %get-tuple-element.131), channel_id=1, source_target_pairs={{0,1},{2,3},{4,5},{6,7},{8,9},{10,11},{12,13},{14,15},{16,17},{18,... | collective-permute-start | bytes 728 | tf_op jit(solution)/shard_map/ppermute | solution.py:21
  139.1 5.2 %collective-permute-start.30 = (f32[1,16,128]{2,1,0:T(8,128)S(1)}, f32[1,16,128]{2,1,0:T(8,128)S(1)}, u32[]{:S(2)}, u32[]{:S(2)}) collective-permute-start(f32[1,16,128]{2,1,0:T(8,128)S(1)} %get-tuple-element.123), channel_id=1, source_target_pairs={{8,0},{16,8},{24,16},{9,1},{17,9},{25,17},{10,2},{18,10},{26,18},{... | collective-permute-start | bytes 24584 | tf_op jit(solution)/shard_map/ppermute | solution.py:23
  144.3 3.2 collective-permute-start.33
  146.2 5.5 %collective-permute-start.32 = (f32[10,1,128]{2,1,0:T(1,128)S(1)}, f32[10,1,128]{2,1,0:T(1,128)S(1)}, u32[]{:S(2)}, u32[]{:S(2)}) collective-permute-start(f32[10,1,128]{2,1,0:T(1,128)S(1)} %get-tuple-element.111), channel_id=1, source_target_pairs={{2,0},{4,2},{6,4},{3,1},{5,3},{7,5},{10,8},{12,10},{14,12},{11,9},... | collective-permute-start | bytes 15368 | tf_op jit(solution)/shard_map/ppermute | solution.py:23
  151.8 8.1 %collective-permute-start.34 = (f32[10,18,1]{2,1,0:T(8,128)S(1)}, f32[10,18,1]{2,1,0:T(8,128)S(1)}, u32[]{:S(2)}, u32[]{:S(2)}) collective-permute-start(f32[10,18,1]{2,1,0:T(8,128)S(1)} %get-tuple-element.98), channel_id=1, source_target_pairs={{1,0},{3,2},{5,4},{7,6},{9,8},{11,10},{13,12},{15,14},{17,16},{19,... | collective-permute-start | bytes 2168 | tf_op jit(solution)/shard_map/ppermute | solution.py:23
  153.1 8.0 %collective-permute-start.35 = (f32[10,18,1]{2,1,0:T(8,128)S(1)}, f32[10,18,1]{2,1,0:T(8,128)S(1)}, u32[]{:S(2)}, u32[]{:S(2)}) collective-permute-start(f32[10,18,1]{2,1,0:T(8,128)S(1)} %get-tuple-element.99), channel_id=1, source_target_pairs={{0,1},{2,3},{4,5},{6,7},{8,9},{10,11},{12,13},{14,15},{16,17},{18,... | collective-permute-start | bytes 2168 | tf_op jit(solution)/shard_map/ppermute | solution.py:21
  163.0 4.2 collective-permute-start.36
  167.2 3.2 collective-permute-start.39
  169.1 5.5 %collective-permute-start.38 = (f32[10,1,128]{2,1,0:T(1,128)S(1)}, f32[10,1,128]{2,1,0:T(1,128)S(1)}, u32[]{:S(2)}, u32[]{:S(2)}) collective-permute-start(f32[10,1,128]{2,1,0:T(1,128)S(1)} %get-tuple-element.109), channel_id=1, source_target_pairs={{2,0},{4,2},{6,4},{3,1},{5,3},{7,5},{10,8},{12,10},{14,12},{11,9},... | collective-permute-start | bytes 15368 | tf_op jit(solution)/shard_map/ppermute | solution.py:23
  174.8 8.0 %collective-permute-start.40 = (f32[10,18,1]{2,1,0:T(8,128)S(1)}, f32[10,18,1]{2,1,0:T(8,128)S(1)}, u32[]{:S(2)}, u32[]{:S(2)}) collective-permute-start(f32[10,18,1]{2,1,0:T(8,128)S(1)} %get-tuple-element.96), channel_id=1, source_target_pairs={{1,0},{3,2},{5,4},{7,6},{9,8},{11,10},{13,12},{15,14},{17,16},{19,... | collective-permute-start | bytes 2168 | tf_op jit(solution)/shard_map/ppermute | solution.py:23
  176.1 8.1 %collective-permute-start.41 = (f32[10,18,1]{2,1,0:T(8,128)S(1)}, f32[10,18,1]{2,1,0:T(8,128)S(1)}, u32[]{:S(2)}, u32[]{:S(2)}) collective-permute-start(f32[10,18,1]{2,1,0:T(8,128)S(1)} %get-tuple-element.97), channel_id=1, source_target_pairs={{0,1},{2,3},{4,5},{6,7},{8,9},{10,11},{12,13},{14,15},{16,17},{18,... | collective-permute-start | bytes 2168 | tf_op jit(solution)/shard_map/ppermute | solution.py:21
  227.1 5.6 %collective-permute-start.42 = (f32[1,16,128]{2,1,0:T(8,128)S(1)}, f32[1,16,128]{2,1,0:T(8,128)S(1)}, u32[]{:S(2)}, u32[]{:S(2)}) collective-permute-start(f32[1,16,128]{2,1,0:T(8,128)S(1)} %get-tuple-element.119), channel_id=1, source_target_pairs={{8,0},{16,8},{24,16},{9,1},{17,9},{25,17},{10,2},{18,10},{26,18},{... | collective-permute-start | bytes 24584 | tf_op jit(solution)/shard_map/ppermute | solution.py:23
  232.7 5.2 %collective-permute-start.45 = (f32[10,1,128]{2,1,0:T(1,128)S(1)}, f32[10,1,128]{2,1,0:T(1,128)S(1)}, u32[]{:S(2)}, u32[]{:S(2)}) collective-permute-start(f32[10,1,128]{2,1,0:T(1,128)S(1)} %get-tuple-element.106), channel_id=1, source_target_pairs={{0,2},{2,4},{4,6},{1,3},{3,5},{5,7},{8,10},{10,12},{12,14},{9,11},... | collective-permute-start | bytes 15368 | tf_op jit(solution)/shard_map/ppermute | solution.py:21
  236.6 5.5 %collective-permute-start.44 = (f32[10,1,128]{2,1,0:T(1,128)S(1)}, f32[10,1,128]{2,1,0:T(1,128)S(1)}, u32[]{:S(2)}, u32[]{:S(2)}) collective-permute-start(f32[10,1,128]{2,1,0:T(1,128)S(1)} %get-tuple-element.107), channel_id=1, source_target_pairs={{2,0},{4,2},{6,4},{3,1},{5,3},{7,5},{10,8},{12,10},{14,12},{11,9},... | collective-permute-start | bytes 15368 | tf_op jit(solution)/shard_map/ppermute | solution.py:23
  242.3 8.1 %collective-permute-start.46 = (f32[10,18,1]{2,1,0:T(8,128)S(1)}, f32[10,18,1]{2,1,0:T(8,128)S(1)}, u32[]{:S(2)}, u32[]{:S(2)}) collective-permute-start(f32[10,18,1]{2,1,0:T(8,128)S(1)} %get-tuple-element.94), channel_id=1, source_target_pairs={{1,0},{3,2},{5,4},{7,6},{9,8},{11,10},{13,12},{15,14},{17,16},{19,... | collective-permute-start | bytes 2168 | tf_op jit(solution)/shard_map/ppermute | solution.py:23
  243.6 8.0 %collective-permute-start.47 = (f32[10,18,1]{2,1,0:T(8,128)S(1)}, f32[10,18,1]{2,1,0:T(8,128)S(1)}, u32[]{:S(2)}, u32[]{:S(2)}) collective-permute-start(f32[10,18,1]{2,1,0:T(8,128)S(1)} %get-tuple-element.95), channel_id=1, source_target_pairs={{0,1},{2,3},{4,5},{6,7},{8,9},{10,11},{12,13},{14,15},{16,17},{18,... | collective-permute-start | bytes 2168 | tf_op jit(solution)/shard_map/ppermute | solution.py:21
  261.5 4.2 collective-permute-start.48
  265.7 3.9 collective-permute-start.51
  268.3 5.5 %collective-permute-start.50 = (f32[6,1,64]{2,1,0:T(1,128)S(1)}, f32[6,1,64]{2,1,0:T(1,128)S(1)}, u32[]{:S(2)}, u32[]{:S(2)}) collective-permute-start(f32[6,1,64]{2,1,0:T(1,128)S(1)} %get-tuple-element.137), channel_id=1, source_target_pairs={{2,0},{4,2},{6,4},{3,1},{5,3},{7,5},{10,8},{12,10},{14,12},{11,9},... | collective-permute-start | bytes 4616 | tf_op jit(solution)/shard_map/ppermute | solution.py:23
  273.9 6.5 %collective-permute-start.52 = (f32[6,10,1]{2,1,0:T(8,128)S(1)}, f32[6,10,1]{2,1,0:T(8,128)S(1)}, u32[]{:S(2)}, u32[]{:S(2)}) collective-permute-start(f32[6,10,1]{2,1,0:T(8,128)S(1)} %get-tuple-element.128), channel_id=1, source_target_pairs={{1,0},{3,2},{5,4},{7,6},{9,8},{11,10},{13,12},{15,14},{17,16},{19,... | collective-permute-start | bytes 728 | tf_op jit(solution)/shard_map/ppermute | solution.py:23
  275.2 6.4 %collective-permute-start.53 = (f32[6,10,1]{2,1,0:T(8,128)S(1)}, f32[6,10,1]{2,1,0:T(8,128)S(1)}, u32[]{:S(2)}, u32[]{:S(2)}) collective-permute-start(f32[6,10,1]{2,1,0:T(8,128)S(1)} %get-tuple-element.129), channel_id=1, source_target_pairs={{0,1},{2,3},{4,5},{6,7},{8,9},{10,11},{12,13},{14,15},{16,17},{18,... | collective-permute-start | bytes 728 | tf_op jit(solution)/shard_map/ppermute | solution.py:21
  284.2 4.9 %collective-permute-start.54 = (f32[1,4,32]{2,1,0:T(4,128)S(1)}, f32[1,4,32]{2,1,0:T(4,128)S(1)}, u32[]{:S(2)}, u32[]{:S(2)}) collective-permute-start(f32[1,4,32]{2,1,0:T(4,128)S(1)} %get-tuple-element.173), channel_id=1, source_target_pairs={{8,0},{16,8},{24,16},{9,1},{17,9},{25,17},{10,2},{18,10},{26,18},{... | collective-permute-start | bytes 1544 | tf_op jit(solution)/shard_map/ppermute | solution.py:23
  291.1 5.5 %collective-permute-start.56 = (f32[4,1,32]{2,1,0:T(1,128)S(1)}, f32[4,1,32]{2,1,0:T(1,128)S(1)}, u32[]{:S(2)}, u32[]{:S(2)}) collective-permute-start(f32[4,1,32]{2,1,0:T(1,128)S(1)} %get-tuple-element.161), channel_id=1, source_target_pairs={{2,0},{4,2},{6,4},{3,1},{5,3},{7,5},{10,8},{12,10},{14,12},{11,9},... | collective-permute-start | bytes 1544 | tf_op jit(solution)/shard_map/ppermute | solution.py:23
  296.6 5.8 %collective-permute-start.58 = (f32[4,6,1]{2,1,0:T(8,128)S(1)}, f32[4,6,1]{2,1,0:T(8,128)S(1)}, u32[]{:S(2)}, u32[]{:S(2)}) collective-permute-start(f32[4,6,1]{2,1,0:T(8,128)S(1)} %get-tuple-element.146), channel_id=1, source_target_pairs={{1,0},{3,2},{5,4},{7,6},{9,8},{11,10},{13,12},{15,14},{17,16},{19,... | collective-permute-start | bytes 296 | tf_op jit(solution)/shard_map/ppermute | solution.py:23
  297.9 6.0 %collective-permute-start.59 = (f32[4,6,1]{2,1,0:T(8,128)S(1)}, f32[4,6,1]{2,1,0:T(8,128)S(1)}, u32[]{:S(2)}, u32[]{:S(2)}) collective-permute-start(f32[4,6,1]{2,1,0:T(8,128)S(1)} %get-tuple-element.147), channel_id=1, source_target_pairs={{0,1},{2,3},{4,5},{6,7},{8,9},{10,11},{12,13},{14,15},{16,17},{18,... | collective-permute-start | bytes 296 | tf_op jit(solution)/shard_map/ppermute | solution.py:21
  305.7 5.2 %collective-permute-start.60 = (f32[1,4,32]{2,1,0:T(4,128)S(1)}, f32[1,4,32]{2,1,0:T(4,128)S(1)}, u32[]{:S(2)}, u32[]{:S(2)}) collective-permute-start(f32[1,4,32]{2,1,0:T(4,128)S(1)} %get-tuple-element.171), channel_id=1, source_target_pairs={{8,0},{16,8},{24,16},{9,1},{17,9},{25,17},{10,2},{18,10},{26,18},{... | collective-permute-start | bytes 1544 | tf_op jit(solution)/shard_map/ppermute | solution.py:23
  312.8 5.5 %collective-permute-start.62 = (f32[4,1,32]{2,1,0:T(1,128)S(1)}, f32[4,1,32]{2,1,0:T(1,128)S(1)}, u32[]{:S(2)}, u32[]{:S(2)}) collective-permute-start(f32[4,1,32]{2,1,0:T(1,128)S(1)} %get-tuple-element.159), channel_id=1, source_target_pairs={{2,0},{4,2},{6,4},{3,1},{5,3},{7,5},{10,8},{12,10},{14,12},{11,9},... | collective-permute-start | bytes 1544 | tf_op jit(solution)/shard_map/ppermute | solution.py:23
  318.3 5.8 %collective-permute-start.64 = (f32[4,6,1]{2,1,0:T(8,128)S(1)}, f32[4,6,1]{2,1,0:T(8,128)S(1)}, u32[]{:S(2)}, u32[]{:S(2)}) collective-permute-start(f32[4,6,1]{2,1,0:T(8,128)S(1)} %get-tuple-element.144), channel_id=1, source_target_pairs={{1,0},{3,2},{5,4},{7,6},{9,8},{11,10},{13,12},{15,14},{17,16},{19,... | collective-permute-start | bytes 296 | tf_op jit(solution)/shard_map/ppermute | solution.py:23
  319.6 6.0 %collective-permute-start.65 = (f32[4,6,1]{2,1,0:T(8,128)S(1)}, f32[4,6,1]{2,1,0:T(8,128)S(1)}, u32[]{:S(2)}, u32[]{:S(2)}) collective-permute-start(f32[4,6,1]{2,1,0:T(8,128)S(1)} %get-tuple-element.145), channel_id=1, source_target_pairs={{0,1},{2,3},{4,5},{6,7},{8,9},{10,11},{12,13},{14,15},{16,17},{18,... | collective-permute-start | bytes 296 | tf_op jit(solution)/shard_map/ppermute | solution.py:21
  327.8 5.2 %collective-permute-start.66 = (f32[1,8,64]{2,1,0:T(8,128)S(1)}, f32[1,8,64]{2,1,0:T(8,128)S(1)}, u32[]{:S(2)}, u32[]{:S(2)}) collective-permute-start(f32[1,8,64]{2,1,0:T(8,128)S(1)} %get-tuple-element.143), channel_id=1, source_target_pairs={{8,0},{16,8},{24,16},{9,1},{17,9},{25,17},{10,2},{18,10},{26,18},{... | collective-permute-start | bytes 6152 | tf_op jit(solution)/shard_map/ppermute | solution.py:23
  334.9 5.5 %collective-permute-start.68 = (f32[6,1,64]{2,1,0:T(1,128)S(1)}, f32[6,1,64]{2,1,0:T(1,128)S(1)}, u32[]{:S(2)}, u32[]{:S(2)}) collective-permute-start(f32[6,1,64]{2,1,0:T(1,128)S(1)} %get-tuple-element.135), channel_id=1, source_target_pairs={{2,0},{4,2},{6,4},{3,1},{5,3},{7,5},{10,8},{12,10},{14,12},{11,9},... | collective-permute-start | bytes 4616 | tf_op jit(solution)/shard_map/ppermute | solution.py:23
  340.5 6.5 %collective-permute-start.70 = (f32[6,10,1]{2,1,0:T(8,128)S(1)}, f32[6,10,1]{2,1,0:T(8,128)S(1)}, u32[]{:S(2)}, u32[]{:S(2)}) collective-permute-start(f32[6,10,1]{2,1,0:T(8,128)S(1)} %get-tuple-element.126), channel_id=1, source_target_pairs={{1,0},{3,2},{5,4},{7,6},{9,8},{11,10},{13,12},{15,14},{17,16},{19,... | collective-permute-start | bytes 728 | tf_op jit(solution)/shard_map/ppermute | solution.py:23
  341.8 6.4 %collective-permute-start.71 = (f32[6,10,1]{2,1,0:T(8,128)S(1)}, f32[6,10,1]{2,1,0:T(8,128)S(1)}, u32[]{:S(2)}, u32[]{:S(2)}) collective-permute-start(f32[6,10,1]{2,1,0:T(8,128)S(1)} %get-tuple-element.127), channel_id=1, source_target_pairs={{0,1},{2,3},{4,5},{6,7},{8,9},{10,11},{12,13},{14,15},{16,17},{18,... | collective-permute-start | bytes 728 | tf_op jit(solution)/shard_map/ppermute | solution.py:21
  356.5 5.2 %collective-permute-start.72 = (f32[1,16,128]{2,1,0:T(8,128)S(1)}, f32[1,16,128]{2,1,0:T(8,128)S(1)}, u32[]{:S(2)}, u32[]{:S(2)}) collective-permute-start(f32[1,16,128]{2,1,0:T(8,128)S(1)} %get-tuple-element.117), channel_id=1, source_target_pairs={{8,0},{16,8},{24,16},{9,1},{17,9},{25,17},{10,2},{18,10},{26,18},{... | collective-permute-start | bytes 24584 | tf_op jit(solution)/shard_map/ppermute | solution.py:23
  363.7 5.5 %collective-permute-start.74 = (f32[10,1,128]{2,1,0:T(1,128)S(1)}, f32[10,1,128]{2,1,0:T(1,128)S(1)}, u32[]{:S(2)}, u32[]{:S(2)}) collective-permute-start(f32[10,1,128]{2,1,0:T(1,128)S(1)} %get-tuple-element.105), channel_id=1, source_target_pairs={{2,0},{4,2},{6,4},{3,1},{5,3},{7,5},{10,8},{12,10},{14,12},{11,9},... | collective-permute-start | bytes 15368 | tf_op jit(solution)/shard_map/ppermute | solution.py:23
  369.3 8.1 %collective-permute-start.76 = (f32[10,18,1]{2,1,0:T(8,128)S(1)}, f32[10,18,1]{2,1,0:T(8,128)S(1)}, u32[]{:S(2)}, u32[]{:S(2)}) collective-permute-start(f32[10,18,1]{2,1,0:T(8,128)S(1)} %get-tuple-element.92), channel_id=1, source_target_pairs={{1,0},{3,2},{5,4},{7,6},{9,8},{11,10},{13,12},{15,14},{17,16},{19,... | collective-permute-start | bytes 2168 | tf_op jit(solution)/shard_map/ppermute | solution.py:23
  370.6 8.0 %collective-permute-start.77 = (f32[10,18,1]{2,1,0:T(8,128)S(1)}, f32[10,18,1]{2,1,0:T(8,128)S(1)}, u32[]{:S(2)}, u32[]{:S(2)}) collective-permute-start(f32[10,18,1]{2,1,0:T(8,128)S(1)} %get-tuple-element.93), channel_id=1, source_target_pairs={{0,1},{2,3},{4,5},{6,7},{8,9},{10,11},{12,13},{14,15},{16,17},{18,... | collective-permute-start | bytes 2168 | tf_op jit(solution)/shard_map/ppermute | solution.py:21
  380.5 4.2 collective-permute-start.78
  386.6 5.5 %collective-permute-start.80 = (f32[10,1,128]{2,1,0:T(1,128)S(1)}, f32[10,1,128]{2,1,0:T(1,128)S(1)}, u32[]{:S(2)}, u32[]{:S(2)}) collective-permute-start(f32[10,1,128]{2,1,0:T(1,128)S(1)} %get-tuple-element.103), channel_id=1, source_target_pairs={{2,0},{4,2},{6,4},{3,1},{5,3},{7,5},{10,8},{12,10},{14,12},{11,9},... | collective-permute-start | bytes 15368 | tf_op jit(solution)/shard_map/ppermute | solution.py:23
  392.2 8.0 %collective-permute-start.82 = (f32[10,18,1]{2,1,0:T(8,128)S(1)}, f32[10,18,1]{2,1,0:T(8,128)S(1)}, u32[]{:S(2)}, u32[]{:S(2)}) collective-permute-start(f32[10,18,1]{2,1,0:T(8,128)S(1)} %get-tuple-element.90), channel_id=1, source_target_pairs={{1,0},{3,2},{5,4},{7,6},{9,8},{11,10},{13,12},{15,14},{17,16},{19,... | collective-permute-start | bytes 2168 | tf_op jit(solution)/shard_map/ppermute | solution.py:23
  393.5 8.1 %collective-permute-start.83 = (f32[10,18,1]{2,1,0:T(8,128)S(1)}, f32[10,18,1]{2,1,0:T(8,128)S(1)}, u32[]{:S(2)}, u32[]{:S(2)}) collective-permute-start(f32[10,18,1]{2,1,0:T(8,128)S(1)} %get-tuple-element.91), channel_id=1, source_target_pairs={{0,1},{2,3},{4,5},{6,7},{8,9},{10,11},{12,13},{14,15},{16,17},{18,... | collective-permute-start | bytes 2168 | tf_op jit(solution)/shard_map/ppermute | solution.py:21
  (20 other events, 61.5 us)
where the time goes:
time: 450 us; the launch traced here: 447 us
  starting transfers between devices  177 us (39%)
  waiting for transfers between devices  142 us (32%)
  blocking collectives  79.2 us (18%)
  local copies, waits for them, and re-layouts  28.4 us (6%)
  other arithmetic  13.1 us (3%)
  between operations  7.66 us (2%)
    ppermute x42, waiting for transfers between devices, padded_2(): lax.ppermute(head, axis, [((i + 1) % count, i) for i in range(ends)])  124 us
    ppermute x42, starting transfers between devices, padded_2(): lax.ppermute(tail, axis, [(i, (i + 1) % count) for i in range(ends)])  122 us
    psum x2, blocking collectives, joint_sums(): lax.psum((jnp.sum(residual * precond), jnp.sum(precond * precond_image)),...  79.2 us
    ppermute x42, starting transfers between devices, padded_2(): lax.ppermute(head, axis, [((i + 1) % count, i) for i in range(ends)])  54.2 us
    ppermute x42, waiting for transfers between devices, padded_2(): lax.ppermute(tail, axis, [(i, (i + 1) % count) for i in range(ends)])  18.2 us
    reshape x4, local copies, waits for them, and re-layouts, restrict(): field.reshape(sx // 2, 2, sy // 2, 2, sz // 2, 2)  12.1 us
  transfers between devices with their start and end apart: 84, of which 52 were waited for; matrix products, arithmetic and copies ran while one was open for 0% of the time, Pallas kernels for 0%

commit v1 on v0

--- a/solution.py
+++ b/solution.py
@@ -76,7 +76,8 @@
 
 def joint_sums(residual, precond, precond_image):
     return lax.psum(
-        (jnp.sum(residual * precond), jnp.sum(precond * precond_image)), ("gx", "gy", "gz")
+        lax.psum((jnp.sum(residual * precond), jnp.sum(precond * precond_image)), ("gy", "gz")),
+        "gx",
     )
 
 

time: 450 us -> 420 us (0.933)
  blocking collectives: 79.2 us -> 53.1 us
    psum x2, blocking collectives: 79.2 us -> 40.5 us  [joint_sums(): lax.psum((jnp.sum(residual * precond), jnp.sum(precond * precond_image)),...]
    psum x0 -> x2, blocking collectives: none -> 12.6 us  [joint_sums(): lax.psum(lax.psum((jnp.sum(residual * precond), jnp.sum(precond * precond...]
where the time goes in v1:
time: 420 us; the launch traced here: 417 us
  starting transfers between devices  174 us (41%)
  waiting for transfers between devices  140 us (33%)
  blocking collectives  53.1 us (13%)
  local copies, waits for them, and re-layouts  28.5 us (7%)
  other arithmetic  13.1 us (3%)
  between operations  7.91 us (2%)
    ppermute x42, waiting for transfers between devices, padded_2(): lax.ppermute(head, axis, [((i + 1) % count, i) for i in range(ends)])  122 us
    ppermute x42, starting transfers between devices, padded_2(): lax.ppermute(tail, axis, [(i, (i + 1) % count) for i in range(ends)])  120 us
    ppermute x42, starting transfers between devices, padded_2(): lax.ppermute(head, axis, [((i + 1) % count, i) for i in range(ends)])  54.4 us
    psum x2, blocking collectives, joint_sums(): lax.psum((jnp.sum(residual * precond), jnp.sum(precond * precond_image)),...  40.5 us
    ppermute x42, waiting for transfers between devices, padded_2(): lax.ppermute(tail, axis, [(i, (i + 1) % count) for i in range(ends)])  18.7 us
    psum x2, blocking collectives, joint_sums(): lax.psum(lax.psum((jnp.sum(residual * precond), jnp.sum(precond * precond...  12.6 us
    reshape x4, local copies, waits for them, and re-layouts, restrict(): field.reshape(sx // 2, 2, sy // 2, 2, sz // 2, 2)  12.2 us
    reshape x4, local copies, waits for them, and re-layouts, prolong(): return spread.reshape(2 * sx, 2 * sy, 2 * sz)  8.54 us
  transfers between devices with their start and end apart: 84, of which 52 were waited for; matrix products, arithmetic and copies ran while one was open for 0% of the time, Pallas kernels for 0%

profile of v1, /device:TPU:0, one launch (start us, length us, event | category | flops | bytes accessed | tf_op | source)
XLA Modules:
  0.0 417.4 jit_solution(4406904910535358577)
XLA Ops:
  5.6 2.4 collective-permute-start.1
  9.3 3.9 collective-permute-done
  13.2 3.5 collective-permute-start.3
  18.0 4.2 %collective-permute-done.2 = f32[10,1,128]{2,1,0:T(1,128)S(1)} collective-permute-done((f32[10,1,128]{2,1,0:T(1,128)S(1)}, f32[10,1,128]{2,1,0:T(1,128)S(1)}, u32[]{:S(2)}, u32[]{:S(2)}) %collective-permute-start.2) | collective-permute-done | bytes 5152 | tf_op jit(solution)/shard_map/ppermute | solution.py:23
  23.6 4.6 %collective-permute-start.5 = (f32[10,18,1]{2,1,0:T(8,128)S(1)}, f32[10,18,1]{2,1,0:T(8,128)S(1)}, u32[]{:S(2)}, u32[]{:S(2)}) collective-permute-start(f32[10,18,1]{2,1,0:T(8,128)S(1)} %get-tuple-element.105), channel_id=1, source_target_pairs={{0,1},{2,3},{4,5},{6,7},{8,9},{10,11},{12,13},{14,15},{16,17},{18,... | collective-permute-start | bytes 2168 | tf_op jit(solution)/shard_map/ppermute | solution.py:21
  28.2 2.2 collective-permute-done.4
  31.7 5.6 %reshape.240 = f32[4,2,8,2,64,2]{5,4,3,2,1,0:T(8,128)} reshape(f32[8,16,128]{2,1,0:T(8,128)S(1)} %fusion.39) | data formatting | bytes 131072 | tf_op jit(solution)/shard_map/reshape | solution.py:44
  37.3 2.5 reduce_sum.72
  42.9 2.9 collective-permute-done.6
  45.8 3.5 collective-permute-start.9
  50.6 4.2 %collective-permute-done.8 = f32[6,1,64]{2,1,0:T(1,128)S(1)} collective-permute-done((f32[6,1,64]{2,1,0:T(1,128)S(1)}, f32[6,1,64]{2,1,0:T(1,128)S(1)}, u32[]{:S(2)}, u32[]{:S(2)}) %collective-permute-start.8) | collective-permute-done | bytes 1568 | tf_op jit(solution)/shard_map/ppermute | solution.py:23
  56.2 4.5 %collective-permute-start.11 = (f32[6,10,1]{2,1,0:T(8,128)S(1)}, f32[6,10,1]{2,1,0:T(8,128)S(1)}, u32[]{:S(2)}, u32[]{:S(2)}) collective-permute-start(f32[6,10,1]{2,1,0:T(8,128)S(1)} %get-tuple-element.137), channel_id=1, source_target_pairs={{0,1},{2,3},{4,5},{6,7},{8,9},{10,11},{12,13},{14,15},{16,17},{18,... | collective-permute-start | bytes 728 | tf_op jit(solution)/shard_map/ppermute | solution.py:21
  66.5 3.6 collective-permute-done.12
  70.1 3.5 collective-permute-start.15
  74.9 4.2 collective-permute-done.14
  80.5 4.5 %collective-permute-start.17 = (f32[4,6,1]{2,1,0:T(8,128)S(1)}, f32[4,6,1]{2,1,0:T(8,128)S(1)}, u32[]{:S(2)}, u32[]{:S(2)}) collective-permute-start(f32[4,6,1]{2,1,0:T(8,128)S(1)} %get-tuple-element.159), channel_id=1, source_target_pairs={{0,1},{2,3},{4,5},{6,7},{8,9},{10,11},{12,13},{14,15},{16,17},{18,... | collective-permute-start | bytes 296 | tf_op jit(solution)/shard_map/ppermute | solution.py:21
  89.5 3.8 collective-permute-done.18
  96.6 4.2 collective-permute-done.20
  102.2 4.5 %collective-permute-start.23 = (f32[4,6,1]{2,1,0:T(8,128)S(1)}, f32[4,6,1]{2,1,0:T(8,128)S(1)}, u32[]{:S(2)}, u32[]{:S(2)}) collective-permute-start(f32[4,6,1]{2,1,0:T(8,128)S(1)} %get-tuple-element.157), channel_id=1, source_target_pairs={{0,1},{2,3},{4,5},{6,7},{8,9},{10,11},{12,13},{14,15},{16,17},{18,... | collective-permute-start | bytes 296 | tf_op jit(solution)/shard_map/ppermute | solution.py:21
  111.7 3.8 collective-permute-done.24
  118.8 4.2 %collective-permute-done.26 = f32[6,1,64]{2,1,0:T(1,128)S(1)} collective-permute-done((f32[6,1,64]{2,1,0:T(1,128)S(1)}, f32[6,1,64]{2,1,0:T(1,128)S(1)}, u32[]{:S(2)}, u32[]{:S(2)}) %collective-permute-start.26) | collective-permute-done | bytes 1568 | tf_op jit(solution)/shard_map/ppermute | solution.py:23
  124.4 4.5 %collective-permute-start.29 = (f32[6,10,1]{2,1,0:T(8,128)S(1)}, f32[6,10,1]{2,1,0:T(8,128)S(1)}, u32[]{:S(2)}, u32[]{:S(2)}) collective-permute-start(f32[6,10,1]{2,1,0:T(8,128)S(1)} %get-tuple-element.135), channel_id=1, source_target_pairs={{0,1},{2,3},{4,5},{6,7},{8,9},{10,11},{12,13},{14,15},{16,17},{18,... | collective-permute-start | bytes 728 | tf_op jit(solution)/shard_map/ppermute | solution.py:21
  130.8 2.6 broadcast_in_dim.43
  133.4 4.0 reshape.243
  140.4 3.9 collective-permute-done.30
  147.5 4.2 %collective-permute-done.32 = f32[10,1,128]{2,1,0:T(1,128)S(1)} collective-permute-done((f32[10,1,128]{2,1,0:T(1,128)S(1)}, f32[10,1,128]{2,1,0:T(1,128)S(1)}, u32[]{:S(2)}, u32[]{:S(2)}) %collective-permute-start.32) | collective-permute-done | bytes 5152 | tf_op jit(solution)/shard_map/ppermute | solution.py:23
  153.2 4.6 %collective-permute-start.35 = (f32[10,18,1]{2,1,0:T(8,128)S(1)}, f32[10,18,1]{2,1,0:T(8,128)S(1)}, u32[]{:S(2)}, u32[]{:S(2)}) collective-permute-start(f32[10,18,1]{2,1,0:T(8,128)S(1)} %get-tuple-element.103), channel_id=1, source_target_pairs={{0,1},{2,3},{4,5},{6,7},{8,9},{10,11},{12,13},{14,15},{16,17},{18,... | collective-permute-start | bytes 2168 | tf_op jit(solution)/shard_map/ppermute | solution.py:21
  157.7 2.2 collective-permute-done.34
  164.4 2.9 collective-permute-done.36
  170.5 4.2 %collective-permute-done.38 = f32[10,1,128]{2,1,0:T(1,128)S(1)} collective-permute-done((f32[10,1,128]{2,1,0:T(1,128)S(1)}, f32[10,1,128]{2,1,0:T(1,128)S(1)}, u32[]{:S(2)}, u32[]{:S(2)}) %collective-permute-start.38) | collective-permute-done | bytes 5152 | tf_op jit(solution)/shard_map/ppermute | solution.py:23
  176.1 4.6 %collective-permute-start.41 = (f32[10,18,1]{2,1,0:T(8,128)S(1)}, f32[10,18,1]{2,1,0:T(8,128)S(1)}, u32[]{:S(2)}, u32[]{:S(2)}) collective-permute-start(f32[10,18,1]{2,1,0:T(8,128)S(1)} %get-tuple-element.101), channel_id=1, source_target_pairs={{0,1},{2,3},{4,5},{6,7},{8,9},{10,11},{12,13},{14,15},{16,17},{18,... | collective-permute-start | bytes 2168 | tf_op jit(solution)/shard_map/ppermute | solution.py:21
  180.7 2.1 collective-permute-done.40
  184.9 20.2 %all-reduce.1 = (f32[]{:T(128)}, f32[]{:T(128)}) all-reduce(f32[]{:T(128)} %get-tuple-element.81, f32[]{:T(128)} %get-tuple-element.80), channel_id=1, replica_groups=mesh['gx'=4,'gy'=4,'gz'=2] {'gy','gz'}, use_global_device_ids=true, to_apply=%region_3.4 | all-reduce | flops 2 | bytes 16 | tf_op jit(solution)/shard_map/psum | solution.py:79
  205.1 6.3 %all-reduce.3 = (f32[]{:T(128)}, f32[]{:T(128)}) all-reduce(f32[]{:T(128)} %get-tuple-element.84, f32[]{:T(128)} %get-tuple-element.85), channel_id=1, replica_groups=mesh['gx'=4,'gy'=4,'gz'=2] {'gx'}, use_global_device_ids=true, to_apply=%region_4.5 | all-reduce | flops 2 | bytes 16 | tf_op jit(solution)/shard_map/psum | solution.py:78
  215.8 2.7 collective-permute-done.42
  221.2 4.2 %collective-permute-done.44 = f32[10,1,128]{2,1,0:T(1,128)S(1)} collective-permute-done((f32[10,1,128]{2,1,0:T(1,128)S(1)}, f32[10,1,128]{2,1,0:T(1,128)S(1)}, u32[]{:S(2)}, u32[]{:S(2)}) %collective-permute-start.44) | collective-permute-done | bytes 5152 | tf_op jit(solution)/shard_map/ppermute | solution.py:23
  226.8 4.6 %collective-permute-start.47 = (f32[10,18,1]{2,1,0:T(8,128)S(1)}, f32[10,18,1]{2,1,0:T(8,128)S(1)}, u32[]{:S(2)}, u32[]{:S(2)}) collective-permute-start(f32[10,18,1]{2,1,0:T(8,128)S(1)} %get-tuple-element.99), channel_id=1, source_target_pairs={{0,1},{2,3},{4,5},{6,7},{8,9},{10,11},{12,13},{14,15},{16,17},{18,... | collective-permute-start | bytes 2168 | tf_op jit(solution)/shard_map/ppermute | solution.py:21
  235.2 5.6 %reshape.244 = f32[4,2,8,2,64,2]{5,4,3,2,1,0:T(8,128)} reshape(f32[8,16,128]{2,1,0:T(8,128)S(1)} %fusion.17) | data formatting | bytes 131072 | tf_op jit(solution)/shard_map/reshape | solution.py:44
  240.8 2.5 reduce_sum.76
  246.7 2.3 collective-permute-done.48
  252.0 4.2 %collective-permute-done.50 = f32[6,1,64]{2,1,0:T(1,128)S(1)} collective-permute-done((f32[6,1,64]{2,1,0:T(1,128)S(1)}, f32[6,1,64]{2,1,0:T(1,128)S(1)}, u32[]{:S(2)}, u32[]{:S(2)}) %collective-permute-start.50) | collective-permute-done | bytes 1568 | tf_op jit(solution)/shard_map/ppermute | solution.py:23
  257.5 4.5 %collective-permute-start.53 = (f32[6,10,1]{2,1,0:T(8,128)S(1)}, f32[6,10,1]{2,1,0:T(8,128)S(1)}, u32[]{:S(2)}, u32[]{:S(2)}) collective-permute-start(f32[6,10,1]{2,1,0:T(8,128)S(1)} %get-tuple-element.133), channel_id=1, source_target_pairs={{0,1},{2,3},{4,5},{6,7},{8,9},{10,11},{12,13},{14,15},{16,17},{18,... | collective-permute-start | bytes 728 | tf_op jit(solution)/shard_map/ppermute | solution.py:21
  267.9 3.6 collective-permute-done.54
  271.5 2.7 collective-permute-start.57
  275.7 4.0 collective-permute-done.56
  281.0 4.5 %collective-permute-start.59 = (f32[4,6,1]{2,1,0:T(8,128)S(1)}, f32[4,6,1]{2,1,0:T(8,128)S(1)}, u32[]{:S(2)}, u32[]{:S(2)}) collective-permute-start(f32[4,6,1]{2,1,0:T(8,128)S(1)} %get-tuple-element.151), channel_id=1, source_target_pairs={{0,1},{2,3},{4,5},{6,7},{8,9},{10,11},{12,13},{14,15},{16,17},{18,... | collective-permute-start | bytes 296 | tf_op jit(solution)/shard_map/ppermute | solution.py:21
  290.1 3.8 collective-permute-done.60
  297.2 4.2 collective-permute-done.62
  302.8 4.5 %collective-permute-start.65 = (f32[4,6,1]{2,1,0:T(8,128)S(1)}, f32[4,6,1]{2,1,0:T(8,128)S(1)}, u32[]{:S(2)}, u32[]{:S(2)}) collective-permute-start(f32[4,6,1]{2,1,0:T(8,128)S(1)} %get-tuple-element.149), channel_id=1, source_target_pairs={{0,1},{2,3},{4,5},{6,7},{8,9},{10,11},{12,13},{14,15},{16,17},{18,... | collective-permute-start | bytes 296 | tf_op jit(solution)/shard_map/ppermute | solution.py:21
  312.3 3.8 collective-permute-done.66
  319.4 4.2 %collective-permute-done.68 = f32[6,1,64]{2,1,0:T(1,128)S(1)} collective-permute-done((f32[6,1,64]{2,1,0:T(1,128)S(1)}, f32[6,1,64]{2,1,0:T(1,128)S(1)}, u32[]{:S(2)}, u32[]{:S(2)}) %collective-permute-start.68) | collective-permute-done | bytes 1568 | tf_op jit(solution)/shard_map/ppermute | solution.py:23
  324.9 4.5 %collective-permute-start.71 = (f32[6,10,1]{2,1,0:T(8,128)S(1)}, f32[6,10,1]{2,1,0:T(8,128)S(1)}, u32[]{:S(2)}, u32[]{:S(2)}) collective-permute-start(f32[6,10,1]{2,1,0:T(8,128)S(1)} %get-tuple-element.131), channel_id=1, source_target_pairs={{0,1},{2,3},{4,5},{6,7},{8,9},{10,11},{12,13},{14,15},{16,17},{18,... | collective-permute-start | bytes 728 | tf_op jit(solution)/shard_map/ppermute | solution.py:21
  331.4 2.6 broadcast_in_dim.45
  334.0 4.0 reshape.247
  341.0 3.9 collective-permute-done.72
  348.1 4.2 %collective-permute-done.74 = f32[10,1,128]{2,1,0:T(1,128)S(1)} collective-permute-done((f32[10,1,128]{2,1,0:T(1,128)S(1)}, f32[10,1,128]{2,1,0:T(1,128)S(1)}, u32[]{:S(2)}, u32[]{:S(2)}) %collective-permute-start.74) | collective-permute-done | bytes 5152 | tf_op jit(solution)/shard_map/ppermute | solution.py:23
  353.7 4.6 %collective-permute-start.77 = (f32[10,18,1]{2,1,0:T(8,128)S(1)}, f32[10,18,1]{2,1,0:T(8,128)S(1)}, u32[]{:S(2)}, u32[]{:S(2)}) collective-permute-start(f32[10,18,1]{2,1,0:T(8,128)S(1)} %get-tuple-element.97), channel_id=1, source_target_pairs={{0,1},{2,3},{4,5},{6,7},{8,9},{10,11},{12,13},{14,15},{16,17},{18,... | collective-permute-start | bytes 2168 | tf_op jit(solution)/shard_map/ppermute | solution.py:21
  358.3 2.2 collective-permute-done.76
  364.9 2.9 collective-permute-done.78
  371.1 4.2 %collective-permute-done.80 = f32[10,1,128]{2,1,0:T(1,128)S(1)} collective-permute-done((f32[10,1,128]{2,1,0:T(1,128)S(1)}, f32[10,1,128]{2,1,0:T(1,128)S(1)}, u32[]{:S(2)}, u32[]{:S(2)}) %collective-permute-start.80) | collective-permute-done | bytes 5152 | tf_op jit(solution)/shard_map/ppermute | solution.py:23
  376.7 4.6 %collective-permute-start.83 = (f32[10,18,1]{2,1,0:T(8,128)S(1)}, f32[10,18,1]{2,1,0:T(8,128)S(1)}, u32[]{:S(2)}, u32[]{:S(2)}) collective-permute-start(f32[10,18,1]{2,1,0:T(8,128)S(1)} %get-tuple-element.95), channel_id=1, source_target_pairs={{0,1},{2,3},{4,5},{6,7},{8,9},{10,11},{12,13},{14,15},{16,17},{18,... | collective-permute-start | bytes 2168 | tf_op jit(solution)/shard_map/ppermute | solution.py:21
  381.3 2.1 collective-permute-done.82
  385.5 20.3 %all-reduce = (f32[]{:T(128)}, f32[]{:T(128)}) all-reduce(f32[]{:T(128)} %get-tuple-element.79, f32[]{:T(128)} %get-tuple-element.78), channel_id=1, replica_groups=mesh['gx'=4,'gy'=4,'gz'=2] {'gy','gz'}, use_global_device_ids=true, to_apply=%region_11.12 | all-reduce | flops 2 | bytes 16 | tf_op jit(solution)/shard_map/psum | solution.py:79
  405.8 6.3 %all-reduce.2 = (f32[]{:T(128)}, f32[]{:T(128)}) all-reduce(f32[]{:T(128)} %get-tuple-element.82, f32[]{:T(128)} %get-tuple-element.83), channel_id=1, replica_groups=mesh['gx'=4,'gy'=4,'gz'=2] {'gx'}, use_global_device_ids=true, to_apply=%region_12.13 | all-reduce | flops 2 | bytes 16 | tf_op jit(solution)/shard_map/psum | solution.py:78
  (220 shorter events, 130.5 us)
Async XLA Ops:
  5.6 3.7 collective-permute-start.1
  8.0 5.2 %collective-permute-start = (f32[1,16,128]{2,1,0:T(8,128)S(1)}, f32[1,16,128]{2,1,0:T(8,128)S(1)}, u32[]{:S(2)}, u32[]{:S(2)}) collective-permute-start(f32[1,16,128]{2,1,0:T(8,128)S(1)} %get-tuple-element.129), channel_id=1, source_target_pairs={{8,0},{16,8},{24,16},{9,1},{17,9},{25,17},{10,2},{18,10},{26,18},{... | collective-permute-start | bytes 24584 | tf_op jit(solution)/shard_map/ppermute | solution.py:23
  13.2 4.8 %collective-permute-start.3 = (f32[10,1,128]{2,1,0:T(1,128)S(1)}, f32[10,1,128]{2,1,0:T(1,128)S(1)}, u32[]{:S(2)}, u32[]{:S(2)}) collective-permute-start(f32[10,1,128]{2,1,0:T(1,128)S(1)} %get-tuple-element.116), channel_id=1, source_target_pairs={{0,2},{2,4},{4,6},{1,3},{3,5},{5,7},{8,10},{10,12},{12,14},{9,11},... | collective-permute-start | bytes 15368 | tf_op jit(solution)/shard_map/ppermute | solution.py:21
  16.7 5.5 %collective-permute-start.2 = (f32[10,1,128]{2,1,0:T(1,128)S(1)}, f32[10,1,128]{2,1,0:T(1,128)S(1)}, u32[]{:S(2)}, u32[]{:S(2)}) collective-permute-start(f32[10,1,128]{2,1,0:T(1,128)S(1)} %get-tuple-element.117), channel_id=1, source_target_pairs={{2,0},{4,2},{6,4},{3,1},{5,3},{7,5},{10,8},{12,10},{14,12},{11,9},... | collective-permute-start | bytes 15368 | tf_op jit(solution)/shard_map/ppermute | solution.py:23
  22.3 8.1 %collective-permute-start.4 = (f32[10,18,1]{2,1,0:T(8,128)S(1)}, f32[10,18,1]{2,1,0:T(8,128)S(1)}, u32[]{:S(2)}, u32[]{:S(2)}) collective-permute-start(f32[10,18,1]{2,1,0:T(8,128)S(1)} %get-tuple-element.104), channel_id=1, source_target_pairs={{1,0},{3,2},{5,4},{7,6},{9,8},{11,10},{13,12},{15,14},{17,16},{19,... | collective-permute-start | bytes 2168 | tf_op jit(solution)/shard_map/ppermute | solution.py:23
  23.6 8.0 %collective-permute-start.5 = (f32[10,18,1]{2,1,0:T(8,128)S(1)}, f32[10,18,1]{2,1,0:T(8,128)S(1)}, u32[]{:S(2)}, u32[]{:S(2)}) collective-permute-start(f32[10,18,1]{2,1,0:T(8,128)S(1)} %get-tuple-element.105), channel_id=1, source_target_pairs={{0,1},{2,3},{4,5},{6,7},{8,9},{10,11},{12,13},{14,15},{16,17},{18,... | collective-permute-start | bytes 2168 | tf_op jit(solution)/shard_map/ppermute | solution.py:21
  41.6 4.2 %collective-permute-start.6 = (f32[1,8,64]{2,1,0:T(8,128)S(1)}, f32[1,8,64]{2,1,0:T(8,128)S(1)}, u32[]{:S(2)}, u32[]{:S(2)}) collective-permute-start(f32[1,8,64]{2,1,0:T(8,128)S(1)} %get-tuple-element.161), channel_id=1, source_target_pairs={{8,0},{16,8},{24,16},{9,1},{17,9},{25,17},{10,2},{18,10},{26,18},{... | collective-permute-start | bytes 6152 | tf_op jit(solution)/shard_map/ppermute | solution.py:23
  45.8 4.8 %collective-permute-start.9 = (f32[6,1,64]{2,1,0:T(1,128)S(1)}, f32[6,1,64]{2,1,0:T(1,128)S(1)}, u32[]{:S(2)}, u32[]{:S(2)}) collective-permute-start(f32[6,1,64]{2,1,0:T(1,128)S(1)} %get-tuple-element.144), channel_id=1, source_target_pairs={{0,2},{2,4},{4,6},{1,3},{3,5},{5,7},{8,10},{10,12},{12,14},{9,11},... | collective-permute-start | bytes 4616 | tf_op jit(solution)/shard_map/ppermute | solution.py:21
  49.3 5.5 %collective-permute-start.8 = (f32[6,1,64]{2,1,0:T(1,128)S(1)}, f32[6,1,64]{2,1,0:T(1,128)S(1)}, u32[]{:S(2)}, u32[]{:S(2)}) collective-permute-start(f32[6,1,64]{2,1,0:T(1,128)S(1)} %get-tuple-element.145), channel_id=1, source_target_pairs={{2,0},{4,2},{6,4},{3,1},{5,3},{7,5},{10,8},{12,10},{14,12},{11,9},... | collective-permute-start | bytes 4616 | tf_op jit(solution)/shard_map/ppermute | solution.py:23
  54.9 6.5 %collective-permute-start.10 = (f32[6,10,1]{2,1,0:T(8,128)S(1)}, f32[6,10,1]{2,1,0:T(8,128)S(1)}, u32[]{:S(2)}, u32[]{:S(2)}) collective-permute-start(f32[6,10,1]{2,1,0:T(8,128)S(1)} %get-tuple-element.136), channel_id=1, source_target_pairs={{1,0},{3,2},{5,4},{7,6},{9,8},{11,10},{13,12},{15,14},{17,16},{19,... | collective-permute-start | bytes 728 | tf_op jit(solution)/shard_map/ppermute | solution.py:23
  56.2 6.4 %collective-permute-start.11 = (f32[6,10,1]{2,1,0:T(8,128)S(1)}, f32[6,10,1]{2,1,0:T(8,128)S(1)}, u32[]{:S(2)}, u32[]{:S(2)}) collective-permute-start(f32[6,10,1]{2,1,0:T(8,128)S(1)} %get-tuple-element.137), channel_id=1, source_target_pairs={{0,1},{2,3},{4,5},{6,7},{8,9},{10,11},{12,13},{14,15},{16,17},{18,... | collective-permute-start | bytes 728 | tf_op jit(solution)/shard_map/ppermute | solution.py:21
  65.2 4.9 %collective-permute-start.12 = (f32[1,4,32]{2,1,0:T(4,128)S(1)}, f32[1,4,32]{2,1,0:T(4,128)S(1)}, u32[]{:S(2)}, u32[]{:S(2)}) collective-permute-start(f32[1,4,32]{2,1,0:T(4,128)S(1)} %get-tuple-element.181), channel_id=1, source_target_pairs={{8,0},{16,8},{24,16},{9,1},{17,9},{25,17},{10,2},{18,10},{26,18},{... | collective-permute-start | bytes 1544 | tf_op jit(solution)/shard_map/ppermute | solution.py:23
  70.1 4.8 %collective-permute-start.15 = (f32[4,1,32]{2,1,0:T(1,128)S(1)}, f32[4,1,32]{2,1,0:T(1,128)S(1)}, u32[]{:S(2)}, u32[]{:S(2)}) collective-permute-start(f32[4,1,32]{2,1,0:T(1,128)S(1)} %get-tuple-element.168), channel_id=1, source_target_pairs={{0,2},{2,4},{4,6},{1,3},{3,5},{5,7},{8,10},{10,12},{12,14},{9,11},... | collective-permute-start | bytes 1544 | tf_op jit(solution)/shard_map/ppermute | solution.py:21
  73.6 5.5 %collective-permute-start.14 = (f32[4,1,32]{2,1,0:T(1,128)S(1)}, f32[4,1,32]{2,1,0:T(1,128)S(1)}, u32[]{:S(2)}, u32[]{:S(2)}) collective-permute-start(f32[4,1,32]{2,1,0:T(1,128)S(1)} %get-tuple-element.169), channel_id=1, source_target_pairs={{2,0},{4,2},{6,4},{3,1},{5,3},{7,5},{10,8},{12,10},{14,12},{11,9},... | collective-permute-start | bytes 1544 | tf_op jit(solution)/shard_map/ppermute | solution.py:23
  79.2 5.8 %collective-permute-start.16 = (f32[4,6,1]{2,1,0:T(8,128)S(1)}, f32[4,6,1]{2,1,0:T(8,128)S(1)}, u32[]{:S(2)}, u32[]{:S(2)}) collective-permute-start(f32[4,6,1]{2,1,0:T(8,128)S(1)} %get-tuple-element.158), channel_id=1, source_target_pairs={{1,0},{3,2},{5,4},{7,6},{9,8},{11,10},{13,12},{15,14},{17,16},{19,... | collective-permute-start | bytes 296 | tf_op jit(solution)/shard_map/ppermute | solution.py:23
  80.5 6.0 %collective-permute-start.17 = (f32[4,6,1]{2,1,0:T(8,128)S(1)}, f32[4,6,1]{2,1,0:T(8,128)S(1)}, u32[]{:S(2)}, u32[]{:S(2)}) collective-permute-start(f32[4,6,1]{2,1,0:T(8,128)S(1)} %get-tuple-element.159), channel_id=1, source_target_pairs={{0,1},{2,3},{4,5},{6,7},{8,9},{10,11},{12,13},{14,15},{16,17},{18,... | collective-permute-start | bytes 296 | tf_op jit(solution)/shard_map/ppermute | solution.py:21
  88.2 5.2 %collective-permute-start.18 = (f32[1,4,32]{2,1,0:T(4,128)S(1)}, f32[1,4,32]{2,1,0:T(4,128)S(1)}, u32[]{:S(2)}, u32[]{:S(2)}) collective-permute-start(f32[1,4,32]{2,1,0:T(4,128)S(1)} %get-tuple-element.179), channel_id=1, source_target_pairs={{8,0},{16,8},{24,16},{9,1},{17,9},{25,17},{10,2},{18,10},{26,18},{... | collective-permute-start | bytes 1544 | tf_op jit(solution)/shard_map/ppermute | solution.py:23
  95.3 5.5 %collective-permute-start.20 = (f32[4,1,32]{2,1,0:T(1,128)S(1)}, f32[4,1,32]{2,1,0:T(1,128)S(1)}, u32[]{:S(2)}, u32[]{:S(2)}) collective-permute-start(f32[4,1,32]{2,1,0:T(1,128)S(1)} %get-tuple-element.167), channel_id=1, source_target_pairs={{2,0},{4,2},{6,4},{3,1},{5,3},{7,5},{10,8},{12,10},{14,12},{11,9},... | collective-permute-start | bytes 1544 | tf_op jit(solution)/shard_map/ppermute | solution.py:23
  100.9 5.8 %collective-permute-start.22 = (f32[4,6,1]{2,1,0:T(8,128)S(1)}, f32[4,6,1]{2,1,0:T(8,128)S(1)}, u32[]{:S(2)}, u32[]{:S(2)}) collective-permute-start(f32[4,6,1]{2,1,0:T(8,128)S(1)} %get-tuple-element.156), channel_id=1, source_target_pairs={{1,0},{3,2},{5,4},{7,6},{9,8},{11,10},{13,12},{15,14},{17,16},{19,... | collective-permute-start | bytes 296 | tf_op jit(solution)/shard_map/ppermute | solution.py:23
  102.2 6.0 %collective-permute-start.23 = (f32[4,6,1]{2,1,0:T(8,128)S(1)}, f32[4,6,1]{2,1,0:T(8,128)S(1)}, u32[]{:S(2)}, u32[]{:S(2)}) collective-permute-start(f32[4,6,1]{2,1,0:T(8,128)S(1)} %get-tuple-element.157), channel_id=1, source_target_pairs={{0,1},{2,3},{4,5},{6,7},{8,9},{10,11},{12,13},{14,15},{16,17},{18,... | collective-permute-start | bytes 296 | tf_op jit(solution)/shard_map/ppermute | solution.py:21
  110.4 5.2 %collective-permute-start.24 = (f32[1,8,64]{2,1,0:T(8,128)S(1)}, f32[1,8,64]{2,1,0:T(8,128)S(1)}, u32[]{:S(2)}, u32[]{:S(2)}) collective-permute-start(f32[1,8,64]{2,1,0:T(8,128)S(1)} %get-tuple-element.155), channel_id=1, source_target_pairs={{8,0},{16,8},{24,16},{9,1},{17,9},{25,17},{10,2},{18,10},{26,18},{... | collective-permute-start | bytes 6152 | tf_op jit(solution)/shard_map/ppermute | solution.py:23
  117.5 5.5 %collective-permute-start.26 = (f32[6,1,64]{2,1,0:T(1,128)S(1)}, f32[6,1,64]{2,1,0:T(1,128)S(1)}, u32[]{:S(2)}, u32[]{:S(2)}) collective-permute-start(f32[6,1,64]{2,1,0:T(1,128)S(1)} %get-tuple-element.143), channel_id=1, source_target_pairs={{2,0},{4,2},{6,4},{3,1},{5,3},{7,5},{10,8},{12,10},{14,12},{11,9},... | collective-permute-start | bytes 4616 | tf_op jit(solution)/shard_map/ppermute | solution.py:23
  123.1 6.5 %collective-permute-start.28 = (f32[6,10,1]{2,1,0:T(8,128)S(1)}, f32[6,10,1]{2,1,0:T(8,128)S(1)}, u32[]{:S(2)}, u32[]{:S(2)}) collective-permute-start(f32[6,10,1]{2,1,0:T(8,128)S(1)} %get-tuple-element.134), channel_id=1, source_target_pairs={{1,0},{3,2},{5,4},{7,6},{9,8},{11,10},{13,12},{15,14},{17,16},{19,... | collective-permute-start | bytes 728 | tf_op jit(solution)/shard_map/ppermute | solution.py:23
  124.4 6.4 %collective-permute-start.29 = (f32[6,10,1]{2,1,0:T(8,128)S(1)}, f32[6,10,1]{2,1,0:T(8,128)S(1)}, u32[]{:S(2)}, u32[]{:S(2)}) collective-permute-start(f32[6,10,1]{2,1,0:T(8,128)S(1)} %get-tuple-element.135), channel_id=1, source_target_pairs={{0,1},{2,3},{4,5},{6,7},{8,9},{10,11},{12,13},{14,15},{16,17},{18,... | collective-permute-start | bytes 728 | tf_op jit(solution)/shard_map/ppermute | solution.py:21
  139.1 5.2 %collective-permute-start.30 = (f32[1,16,128]{2,1,0:T(8,128)S(1)}, f32[1,16,128]{2,1,0:T(8,128)S(1)}, u32[]{:S(2)}, u32[]{:S(2)}) collective-permute-start(f32[1,16,128]{2,1,0:T(8,128)S(1)} %get-tuple-element.127), channel_id=1, source_target_pairs={{8,0},{16,8},{24,16},{9,1},{17,9},{25,17},{10,2},{18,10},{26,18},{... | collective-permute-start | bytes 24584 | tf_op jit(solution)/shard_map/ppermute | solution.py:23
  144.3 3.2 collective-permute-start.33
  146.2 5.5 %collective-permute-start.32 = (f32[10,1,128]{2,1,0:T(1,128)S(1)}, f32[10,1,128]{2,1,0:T(1,128)S(1)}, u32[]{:S(2)}, u32[]{:S(2)}) collective-permute-start(f32[10,1,128]{2,1,0:T(1,128)S(1)} %get-tuple-element.115), channel_id=1, source_target_pairs={{2,0},{4,2},{6,4},{3,1},{5,3},{7,5},{10,8},{12,10},{14,12},{11,9},... | collective-permute-start | bytes 15368 | tf_op jit(solution)/shard_map/ppermute | solution.py:23
  151.9 8.1 %collective-permute-start.34 = (f32[10,18,1]{2,1,0:T(8,128)S(1)}, f32[10,18,1]{2,1,0:T(8,128)S(1)}, u32[]{:S(2)}, u32[]{:S(2)}) collective-permute-start(f32[10,18,1]{2,1,0:T(8,128)S(1)} %get-tuple-element.102), channel_id=1, source_target_pairs={{1,0},{3,2},{5,4},{7,6},{9,8},{11,10},{13,12},{15,14},{17,16},{19,... | collective-permute-start | bytes 2168 | tf_op jit(solution)/shard_map/ppermute | solution.py:23
  153.2 8.0 %collective-permute-start.35 = (f32[10,18,1]{2,1,0:T(8,128)S(1)}, f32[10,18,1]{2,1,0:T(8,128)S(1)}, u32[]{:S(2)}, u32[]{:S(2)}) collective-permute-start(f32[10,18,1]{2,1,0:T(8,128)S(1)} %get-tuple-element.103), channel_id=1, source_target_pairs={{0,1},{2,3},{4,5},{6,7},{8,9},{10,11},{12,13},{14,15},{16,17},{18,... | collective-permute-start | bytes 2168 | tf_op jit(solution)/shard_map/ppermute | solution.py:21
  163.0 4.2 %collective-permute-start.36 = (f32[1,16,128]{2,1,0:T(8,128)S(1)}, f32[1,16,128]{2,1,0:T(8,128)S(1)}, u32[]{:S(2)}, u32[]{:S(2)}) collective-permute-start(f32[1,16,128]{2,1,0:T(8,128)S(1)} %get-tuple-element.125), channel_id=1, source_target_pairs={{8,0},{16,8},{24,16},{9,1},{17,9},{25,17},{10,2},{18,10},{26,18},{... | collective-permute-start | bytes 24584 | tf_op jit(solution)/shard_map/ppermute | solution.py:23
  167.2 3.2 collective-permute-start.39
  169.2 5.5 %collective-permute-start.38 = (f32[10,1,128]{2,1,0:T(1,128)S(1)}, f32[10,1,128]{2,1,0:T(1,128)S(1)}, u32[]{:S(2)}, u32[]{:S(2)}) collective-permute-start(f32[10,1,128]{2,1,0:T(1,128)S(1)} %get-tuple-element.113), channel_id=1, source_target_pairs={{2,0},{4,2},{6,4},{3,1},{5,3},{7,5},{10,8},{12,10},{14,12},{11,9},... | collective-permute-start | bytes 15368 | tf_op jit(solution)/shard_map/ppermute | solution.py:23
  174.8 8.0 %collective-permute-start.40 = (f32[10,18,1]{2,1,0:T(8,128)S(1)}, f32[10,18,1]{2,1,0:T(8,128)S(1)}, u32[]{:S(2)}, u32[]{:S(2)}) collective-permute-start(f32[10,18,1]{2,1,0:T(8,128)S(1)} %get-tuple-element.100), channel_id=1, source_target_pairs={{1,0},{3,2},{5,4},{7,6},{9,8},{11,10},{13,12},{15,14},{17,16},{19,... | collective-permute-start | bytes 2168 | tf_op jit(solution)/shard_map/ppermute | solution.py:23
  176.1 8.1 %collective-permute-start.41 = (f32[10,18,1]{2,1,0:T(8,128)S(1)}, f32[10,18,1]{2,1,0:T(8,128)S(1)}, u32[]{:S(2)}, u32[]{:S(2)}) collective-permute-start(f32[10,18,1]{2,1,0:T(8,128)S(1)} %get-tuple-element.101), channel_id=1, source_target_pairs={{0,1},{2,3},{4,5},{6,7},{8,9},{10,11},{12,13},{14,15},{16,17},{18,... | collective-permute-start | bytes 2168 | tf_op jit(solution)/shard_map/ppermute | solution.py:21
  214.5 4.0 collective-permute-start.42
  219.9 5.5 %collective-permute-start.44 = (f32[10,1,128]{2,1,0:T(1,128)S(1)}, f32[10,1,128]{2,1,0:T(1,128)S(1)}, u32[]{:S(2)}, u32[]{:S(2)}) collective-permute-start(f32[10,1,128]{2,1,0:T(1,128)S(1)} %get-tuple-element.111), channel_id=1, source_target_pairs={{2,0},{4,2},{6,4},{3,1},{5,3},{7,5},{10,8},{12,10},{14,12},{11,9},... | collective-permute-start | bytes 15368 | tf_op jit(solution)/shard_map/ppermute | solution.py:23
  225.5 7.8 %collective-permute-start.46 = (f32[10,18,1]{2,1,0:T(8,128)S(1)}, f32[10,18,1]{2,1,0:T(8,128)S(1)}, u32[]{:S(2)}, u32[]{:S(2)}) collective-permute-start(f32[10,18,1]{2,1,0:T(8,128)S(1)} %get-tuple-element.98), channel_id=1, source_target_pairs={{1,0},{3,2},{5,4},{7,6},{9,8},{11,10},{13,12},{15,14},{17,16},{19,... | collective-permute-start | bytes 2168 | tf_op jit(solution)/shard_map/ppermute | solution.py:23
  226.8 8.2 %collective-permute-start.47 = (f32[10,18,1]{2,1,0:T(8,128)S(1)}, f32[10,18,1]{2,1,0:T(8,128)S(1)}, u32[]{:S(2)}, u32[]{:S(2)}) collective-permute-start(f32[10,18,1]{2,1,0:T(8,128)S(1)} %get-tuple-element.99), channel_id=1, source_target_pairs={{0,1},{2,3},{4,5},{6,7},{8,9},{10,11},{12,13},{14,15},{16,17},{18,... | collective-permute-start | bytes 2168 | tf_op jit(solution)/shard_map/ppermute | solution.py:21
  243.3 3.3 collective-permute-start.49
  245.4 3.6 collective-permute-start.48
  250.7 5.5 %collective-permute-start.50 = (f32[6,1,64]{2,1,0:T(1,128)S(1)}, f32[6,1,64]{2,1,0:T(1,128)S(1)}, u32[]{:S(2)}, u32[]{:S(2)}) collective-permute-start(f32[6,1,64]{2,1,0:T(1,128)S(1)} %get-tuple-element.141), channel_id=1, source_target_pairs={{2,0},{4,2},{6,4},{3,1},{5,3},{7,5},{10,8},{12,10},{14,12},{11,9},... | collective-permute-start | bytes 4616 | tf_op jit(solution)/shard_map/ppermute | solution.py:23
  256.3 6.5 %collective-permute-start.52 = (f32[6,10,1]{2,1,0:T(8,128)S(1)}, f32[6,10,1]{2,1,0:T(8,128)S(1)}, u32[]{:S(2)}, u32[]{:S(2)}) collective-permute-start(f32[6,10,1]{2,1,0:T(8,128)S(1)} %get-tuple-element.132), channel_id=1, source_target_pairs={{1,0},{3,2},{5,4},{7,6},{9,8},{11,10},{13,12},{15,14},{17,16},{19,... | collective-permute-start | bytes 728 | tf_op jit(solution)/shard_map/ppermute | solution.py:23
  257.5 6.4 %collective-permute-start.53 = (f32[6,10,1]{2,1,0:T(8,128)S(1)}, f32[6,10,1]{2,1,0:T(8,128)S(1)}, u32[]{:S(2)}, u32[]{:S(2)}) collective-permute-start(f32[6,10,1]{2,1,0:T(8,128)S(1)} %get-tuple-element.133), channel_id=1, source_target_pairs={{0,1},{2,3},{4,5},{6,7},{8,9},{10,11},{12,13},{14,15},{16,17},{18,... | collective-permute-start | bytes 728 | tf_op jit(solution)/shard_map/ppermute | solution.py:21
  266.5 4.9 %collective-permute-start.54 = (f32[1,4,32]{2,1,0:T(4,128)S(1)}, f32[1,4,32]{2,1,0:T(4,128)S(1)}, u32[]{:S(2)}, u32[]{:S(2)}) collective-permute-start(f32[1,4,32]{2,1,0:T(4,128)S(1)} %get-tuple-element.177), channel_id=1, source_target_pairs={{8,0},{16,8},{24,16},{9,1},{17,9},{25,17},{10,2},{18,10},{26,18},{... | collective-permute-start | bytes 1544 | tf_op jit(solution)/shard_map/ppermute | solution.py:23
  271.5 4.2 collective-permute-start.57
  274.2 5.5 %collective-permute-start.56 = (f32[4,1,32]{2,1,0:T(1,128)S(1)}, f32[4,1,32]{2,1,0:T(1,128)S(1)}, u32[]{:S(2)}, u32[]{:S(2)}) collective-permute-start(f32[4,1,32]{2,1,0:T(1,128)S(1)} %get-tuple-element.165), channel_id=1, source_target_pairs={{2,0},{4,2},{6,4},{3,1},{5,3},{7,5},{10,8},{12,10},{14,12},{11,9},... | collective-permute-start | bytes 1544 | tf_op jit(solution)/shard_map/ppermute | solution.py:23
  279.8 5.8 %collective-permute-start.58 = (f32[4,6,1]{2,1,0:T(8,128)S(1)}, f32[4,6,1]{2,1,0:T(8,128)S(1)}, u32[]{:S(2)}, u32[]{:S(2)}) collective-permute-start(f32[4,6,1]{2,1,0:T(8,128)S(1)} %get-tuple-element.150), channel_id=1, source_target_pairs={{1,0},{3,2},{5,4},{7,6},{9,8},{11,10},{13,12},{15,14},{17,16},{19,... | collective-permute-start | bytes 296 | tf_op jit(solution)/shard_map/ppermute | solution.py:23
  281.0 6.0 %collective-permute-start.59 = (f32[4,6,1]{2,1,0:T(8,128)S(1)}, f32[4,6,1]{2,1,0:T(8,128)S(1)}, u32[]{:S(2)}, u32[]{:S(2)}) collective-permute-start(f32[4,6,1]{2,1,0:T(8,128)S(1)} %get-tuple-element.151), channel_id=1, source_target_pairs={{0,1},{2,3},{4,5},{6,7},{8,9},{10,11},{12,13},{14,15},{16,17},{18,... | collective-permute-start | bytes 296 | tf_op jit(solution)/shard_map/ppermute | solution.py:21
  288.8 5.2 %collective-permute-start.60 = (f32[1,4,32]{2,1,0:T(4,128)S(1)}, f32[1,4,32]{2,1,0:T(4,128)S(1)}, u32[]{:S(2)}, u32[]{:S(2)}) collective-permute-start(f32[1,4,32]{2,1,0:T(4,128)S(1)} %get-tuple-element.175), channel_id=1, source_target_pairs={{8,0},{16,8},{24,16},{9,1},{17,9},{25,17},{10,2},{18,10},{26,18},{... | collective-permute-start | bytes 1544 | tf_op jit(solution)/shard_map/ppermute | solution.py:23
  295.9 5.5 %collective-permute-start.62 = (f32[4,1,32]{2,1,0:T(1,128)S(1)}, f32[4,1,32]{2,1,0:T(1,128)S(1)}, u32[]{:S(2)}, u32[]{:S(2)}) collective-permute-start(f32[4,1,32]{2,1,0:T(1,128)S(1)} %get-tuple-element.163), channel_id=1, source_target_pairs={{2,0},{4,2},{6,4},{3,1},{5,3},{7,5},{10,8},{12,10},{14,12},{11,9},... | collective-permute-start | bytes 1544 | tf_op jit(solution)/shard_map/ppermute | solution.py:23
  301.5 5.8 %collective-permute-start.64 = (f32[4,6,1]{2,1,0:T(8,128)S(1)}, f32[4,6,1]{2,1,0:T(8,128)S(1)}, u32[]{:S(2)}, u32[]{:S(2)}) collective-permute-start(f32[4,6,1]{2,1,0:T(8,128)S(1)} %get-tuple-element.148), channel_id=1, source_target_pairs={{1,0},{3,2},{5,4},{7,6},{9,8},{11,10},{13,12},{15,14},{17,16},{19,... | collective-permute-start | bytes 296 | tf_op jit(solution)/shard_map/ppermute | solution.py:23
  302.8 6.0 %collective-permute-start.65 = (f32[4,6,1]{2,1,0:T(8,128)S(1)}, f32[4,6,1]{2,1,0:T(8,128)S(1)}, u32[]{:S(2)}, u32[]{:S(2)}) collective-permute-start(f32[4,6,1]{2,1,0:T(8,128)S(1)} %get-tuple-element.149), channel_id=1, source_target_pairs={{0,1},{2,3},{4,5},{6,7},{8,9},{10,11},{12,13},{14,15},{16,17},{18,... | collective-permute-start | bytes 296 | tf_op jit(solution)/shard_map/ppermute | solution.py:21
  311.0 5.2 %collective-permute-start.66 = (f32[1,8,64]{2,1,0:T(8,128)S(1)}, f32[1,8,64]{2,1,0:T(8,128)S(1)}, u32[]{:S(2)}, u32[]{:S(2)}) collective-permute-start(f32[1,8,64]{2,1,0:T(8,128)S(1)} %get-tuple-element.147), channel_id=1, source_target_pairs={{8,0},{16,8},{24,16},{9,1},{17,9},{25,17},{10,2},{18,10},{26,18},{... | collective-permute-start | bytes 6152 | tf_op jit(solution)/shard_map/ppermute | solution.py:23
  318.1 5.5 %collective-permute-start.68 = (f32[6,1,64]{2,1,0:T(1,128)S(1)}, f32[6,1,64]{2,1,0:T(1,128)S(1)}, u32[]{:S(2)}, u32[]{:S(2)}) collective-permute-start(f32[6,1,64]{2,1,0:T(1,128)S(1)} %get-tuple-element.139), channel_id=1, source_target_pairs={{2,0},{4,2},{6,4},{3,1},{5,3},{7,5},{10,8},{12,10},{14,12},{11,9},... | collective-permute-start | bytes 4616 | tf_op jit(solution)/shard_map/ppermute | solution.py:23
  323.7 6.5 %collective-permute-start.70 = (f32[6,10,1]{2,1,0:T(8,128)S(1)}, f32[6,10,1]{2,1,0:T(8,128)S(1)}, u32[]{:S(2)}, u32[]{:S(2)}) collective-permute-start(f32[6,10,1]{2,1,0:T(8,128)S(1)} %get-tuple-element.130), channel_id=1, source_target_pairs={{1,0},{3,2},{5,4},{7,6},{9,8},{11,10},{13,12},{15,14},{17,16},{19,... | collective-permute-start | bytes 728 | tf_op jit(solution)/shard_map/ppermute | solution.py:23
  324.9 6.4 %collective-permute-start.71 = (f32[6,10,1]{2,1,0:T(8,128)S(1)}, f32[6,10,1]{2,1,0:T(8,128)S(1)}, u32[]{:S(2)}, u32[]{:S(2)}) collective-permute-start(f32[6,10,1]{2,1,0:T(8,128)S(1)} %get-tuple-element.131), channel_id=1, source_target_pairs={{0,1},{2,3},{4,5},{6,7},{8,9},{10,11},{12,13},{14,15},{16,17},{18,... | collective-permute-start | bytes 728 | tf_op jit(solution)/shard_map/ppermute | solution.py:21
  339.7 5.2 %collective-permute-start.72 = (f32[1,16,128]{2,1,0:T(8,128)S(1)}, f32[1,16,128]{2,1,0:T(8,128)S(1)}, u32[]{:S(2)}, u32[]{:S(2)}) collective-permute-start(f32[1,16,128]{2,1,0:T(8,128)S(1)} %get-tuple-element.121), channel_id=1, source_target_pairs={{8,0},{16,8},{24,16},{9,1},{17,9},{25,17},{10,2},{18,10},{26,18},{... | collective-permute-start | bytes 24584 | tf_op jit(solution)/shard_map/ppermute | solution.py:23
  346.8 5.5 %collective-permute-start.74 = (f32[10,1,128]{2,1,0:T(1,128)S(1)}, f32[10,1,128]{2,1,0:T(1,128)S(1)}, u32[]{:S(2)}, u32[]{:S(2)}) collective-permute-start(f32[10,1,128]{2,1,0:T(1,128)S(1)} %get-tuple-element.109), channel_id=1, source_target_pairs={{2,0},{4,2},{6,4},{3,1},{5,3},{7,5},{10,8},{12,10},{14,12},{11,9},... | collective-permute-start | bytes 15368 | tf_op jit(solution)/shard_map/ppermute | solution.py:23
  352.4 8.1 %collective-permute-start.76 = (f32[10,18,1]{2,1,0:T(8,128)S(1)}, f32[10,18,1]{2,1,0:T(8,128)S(1)}, u32[]{:S(2)}, u32[]{:S(2)}) collective-permute-start(f32[10,18,1]{2,1,0:T(8,128)S(1)} %get-tuple-element.96), channel_id=1, source_target_pairs={{1,0},{3,2},{5,4},{7,6},{9,8},{11,10},{13,12},{15,14},{17,16},{19,... | collective-permute-start | bytes 2168 | tf_op jit(solution)/shard_map/ppermute | solution.py:23
  353.7 8.0 %collective-permute-start.77 = (f32[10,18,1]{2,1,0:T(8,128)S(1)}, f32[10,18,1]{2,1,0:T(8,128)S(1)}, u32[]{:S(2)}, u32[]{:S(2)}) collective-permute-start(f32[10,18,1]{2,1,0:T(8,128)S(1)} %get-tuple-element.97), channel_id=1, source_target_pairs={{0,1},{2,3},{4,5},{6,7},{8,9},{10,11},{12,13},{14,15},{16,17},{18,... | collective-permute-start | bytes 2168 | tf_op jit(solution)/shard_map/ppermute | solution.py:21
  363.6 4.2 %collective-permute-start.78 = (f32[1,16,128]{2,1,0:T(8,128)S(1)}, f32[1,16,128]{2,1,0:T(8,128)S(1)}, u32[]{:S(2)}, u32[]{:S(2)}) collective-permute-start(f32[1,16,128]{2,1,0:T(8,128)S(1)} %get-tuple-element.119), channel_id=1, source_target_pairs={{8,0},{16,8},{24,16},{9,1},{17,9},{25,17},{10,2},{18,10},{26,18},{... | collective-permute-start | bytes 24584 | tf_op jit(solution)/shard_map/ppermute | solution.py:23
  369.8 5.5 %collective-permute-start.80 = (f32[10,1,128]{2,1,0:T(1,128)S(1)}, f32[10,1,128]{2,1,0:T(1,128)S(1)}, u32[]{:S(2)}, u32[]{:S(2)}) collective-permute-start(f32[10,1,128]{2,1,0:T(1,128)S(1)} %get-tuple-element.107), channel_id=1, source_target_pairs={{2,0},{4,2},{6,4},{3,1},{5,3},{7,5},{10,8},{12,10},{14,12},{11,9},... | collective-permute-start | bytes 15368 | tf_op jit(solution)/shard_map/ppermute | solution.py:23
  375.4 8.0 %collective-permute-start.82 = (f32[10,18,1]{2,1,0:T(8,128)S(1)}, f32[10,18,1]{2,1,0:T(8,128)S(1)}, u32[]{:S(2)}, u32[]{:S(2)}) collective-permute-start(f32[10,18,1]{2,1,0:T(8,128)S(1)} %get-tuple-element.94), channel_id=1, source_target_pairs={{1,0},{3,2},{5,4},{7,6},{9,8},{11,10},{13,12},{15,14},{17,16},{19,... | collective-permute-start | bytes 2168 | tf_op jit(solution)/shard_map/ppermute | solution.py:23
  376.7 8.1 %collective-permute-start.83 = (f32[10,18,1]{2,1,0:T(8,128)S(1)}, f32[10,18,1]{2,1,0:T(8,128)S(1)}, u32[]{:S(2)}, u32[]{:S(2)}) collective-permute-start(f32[10,18,1]{2,1,0:T(8,128)S(1)} %get-tuple-element.95), channel_id=1, source_target_pairs={{0,1},{2,3},{4,5},{6,7},{8,9},{10,11},{12,13},{14,15},{16,17},{18,... | collective-permute-start | bytes 2168 | tf_op jit(solution)/shard_map/ppermute | solution.py:21
  (20 other events, 61.3 us)
